TPU v7x, 512 devices: a whole 4x8x8 slice. The times are simulated.
512 devices in a mesh: vocab: 32 (over x, y), hidden: 16 (over z, core).
Axes of the slice: x: 4, y: 8, z: 8, core: 2. Of those that a mesh axis runs over, the one named last changes fastest.
Arguments:
- token_ids: int32 [16384], P('vocab'), may hold values from 0 to 30719
- table: bfloat16 [30720, 128], P('vocab'), may hold values from -0.125 to 0.125
- projection: bfloat16 [128, 4096], P(None, 'hidden'), may hold values from -0.09375 to 0.09375
- grad_out: bfloat16 [16384, 4096], P('vocab', 'hidden'), may hold values from -6 to 6
Outputs:
- table_grad: float32 [30720, 128], P('vocab', 'hidden')
- projection_grad: float32 [128, 4096], P(None, 'hidden')
All inputs are finite; a program needn't handle non-finite values.
Results may differ from a plain program's by a relative error of at most 0.018.
Values may be sent and summed in bfloat16 or wider, within the bound.
No kernel may reach another device: no remote copies, remote signals or barrier semaphores. Data moves between devices by JAX's collectives and lax.ppermute only.
A program may use at most 64 MiB of HBM per device.

v0:
```python
import jax
import jax.numpy as jnp
from jax import lax
from jax.sharding import PartitionSpec as P


def cut_along(x, dim, peers):
    lengths = x.shape
    blocks = x.reshape(*lengths[:dim], peers, lengths[dim] // peers, *lengths[dim + 1 :])
    return jnp.moveaxis(blocks, dim, 0)


def sent_and_summed(x, axis, dim):
    blocks = cut_along(x, dim, lax.axis_size(axis))
    arrived = lax.all_to_all(blocks, axis, split_axis=0, concat_axis=0, tiled=True)
    return arrived.astype(jnp.float32).sum(axis=0)


def sent_to_all(x, axis):
    peers = lax.axis_size(axis)
    return lax.all_to_all(jnp.broadcast_to(x[None], (peers, *x.shape)), axis, 0, 0, tiled=True)


def laid_out(blocks, dim):
    blocks = jnp.moveaxis(blocks, 0, dim)
    lengths = blocks.shape
    return blocks.reshape(*lengths[:dim], lengths[dim] * lengths[dim + 1], *lengths[dim + 2 :])


def collect(x, axis, dim):
    blocks = sent_to_all(x, axis)
    return laid_out(blocks, dim)


def padded_to(lines, peers):
    spare = -lines.shape[0] % peers
    if not spare:
        return lines
    return jnp.concatenate([lines, jnp.zeros((spare, *lines.shape[1:]), lines.dtype)])


def sum_by_parts(x, axes):
    lines = x.reshape(-1, x.shape[-1])
    padded = padded_to(lines, lax.axis_size(axes))
    whole = collect(sent_and_summed(padded, axes, 0).astype(jnp.bfloat16), axes, 0)
    return lax.slice_in_dim(whole, 0, len(lines)).reshape(x.shape).astype(jnp.float32)


def lookup_rows(token_ids, piece):
    count = piece.shape[0]
    inside = (token_ids >= 0) & (token_ids < count)
    picked = jnp.take(piece, jnp.clip(token_ids, 0, count - 1), axis=0)
    return jnp.where(inside[:, None], picked.astype(jnp.float32), 0.0)


def on_device(token_ids, table, projection, grad_out):
    partial_grad = jnp.dot(grad_out, projection.T, preferred_element_type=jnp.float32)
    rounded = partial_grad.astype(jnp.bfloat16)
    token_grad = sent_and_summed(rounded, "hidden", 1).astype(jnp.bfloat16)
    row_count = table.shape[0]
    width = table.shape[1] // lax.axis_size("hidden")
    columns = lax.dynamic_slice_in_dim(table, lax.axis_index("hidden") * width, width, 1)
    looked = lookup_rows(token_ids, collect(columns, "vocab", 0))
    embedded = collect(looked.astype(jnp.bfloat16), "hidden", 1)
    partial_proj = jnp.dot(embedded.T, grad_out, preferred_element_type=jnp.float32)
    projection_grad = sum_by_parts(partial_proj.astype(jnp.bfloat16), "vocab")
    row_ids = lax.iota(jnp.int32, row_count * lax.axis_size("vocab"))
    one_hot = (row_ids[:, None] == token_ids[None, :]).astype(jnp.bfloat16)
    table_grad = sent_and_summed(
        jnp.dot(one_hot, token_grad, preferred_element_type=jnp.float32).astype(jnp.bfloat16),
        "vocab",
        0,
    )
    return (table_grad, projection_grad)


def solution(mesh):
    placed = (P("vocab"), P("vocab", None), P(None, "hidden"), P("vocab", "hidden"))
    return jax.shard_map(
        on_device,
        mesh=mesh,
        in_specs=placed,
        out_specs=(P("vocab", "hidden"), P(None, "hidden")),
        check_vma=False,
    )
```

profile of v0, /device:TPU:8, one launch (start us, length us, event | category | flops | bytes accessed | tf_op | source)
XLA Modules:
  0.0 129.0 jit_solution(12233188906107637453)
XLA Ops:
  0.6 0.0 copy-start
  0.6 0.0 copy-start.1
  0.7 1.1 constant_dynamic-slice_fusion
  1.8 0.1 copy.12
  1.9 0.9 broadcast_in_dim.47
  2.8 10.2 %all-to-all-start.2 = ((bf16[32,960,8]{1,2,0:T(8,128)(2,1)}), bf16[32,960,8]{1,2,0:T(8,128)(2,1)S(1)}, u32[]{:S(2)}, u32[]{:S(2)}) async-start(bf16[32,960,8]{1,2,0:T(8,128)(2,1)} %broadcast_in_dim.47), calls=%async_computation.2 | async-start | bytes 1048576 | tf_op jit(solution)/shard_map/all_to_all | solution.py:21
  12.9 0.0 copy-done
  12.9 1.7 %fusion.3 = bf16[16,512,8]{1,2,0:T(8,128)(2,1)} fusion(bf16[512,256]{1,0:T(8,128)(2,1)S(1)} %copy-done, bf16[128,256]{1,0:T(8,128)(2,1)} %param.6), kind=kOutput, calls=%fused_computation.6 | convolution fusion | flops 33619968 | bytes 458752 | tf_op jit(solution)/shard_map/dot_general | solution.py:57
  14.7 0.7 compare_and_fusion.1
  15.3 0.7 compare_select_fusion
  16.0 14.5 %all-to-all-done.2 = bf16[32,960,8]{1,2,0:T(8,128)(2,1)S(1)} async-done(((bf16[32,960,8]{1,2,0:T(8,128)(2,1)}), bf16[32,960,8]{1,2,0:T(8,128)(2,1)S(1)}, u32[]{:S(2)}, u32[]{:S(2)}) %all-to-all-start.2) | async-done | bytes 491552 | tf_op jit(solution)/shard_map/all_to_all | solution.py:21
  30.5 10.4 %all-to-all-start = ((bf16[16,512,8]{1,2,0:T(8,128)(2,1)}), bf16[16,512,8]{1,2,0:T(8,128)(2,1)S(1)}, u32[]{:S(2)}, u32[]{:S(2)}) async-start(bf16[16,512,8]{1,2,0:T(8,128)(2,1)} %fusion.3), calls=%async_computation | async-start | bytes 262144 | tf_op jit(solution)/shard_map/all_to_all | solution.py:15
  41.0 5.2 %copy.13 = bf16[32,960,8]{2,1,0:T(8,128)(2,1)} copy(bf16[32,960,8]{1,2,0:T(8,128)(2,1)S(1)} %all-to-all-done.2) | data formatting | bytes 983040 | tf_op jit(solution)/shard_map/all_to_all | solution.py:21
  46.2 5.3 %gather_fusion = bf16[512,8]{1,0:T(8,128)(2,1)S(1)} fusion(bf16[30720,8]{1,0:T(8,128)(2,1)} %bitcast.16, s32[1024]{0:T(1024)S(1)} %pad_clamp_fusion), kind=kCustom, calls=%fused_computation | custom fusion | bytes 18432 | tf_op jit(solution)/shard_map/jit(_take)/gather | solution.py:52
  51.5 0.1 copy.14
  51.6 0.0 all-to-all-done
  51.6 0.7 broadcast_in_dim.51
  52.3 7.2 %all-to-all-start.3 = ((bf16[16,512,8]{1,2,0:T(8,128)(2,1)}), bf16[16,512,8]{1,2,0:T(8,128)(2,1)S(1)}, u32[]{:S(2)}, u32[]{:S(2)}) async-start(bf16[16,512,8]{1,2,0:T(8,128)(2,1)} %broadcast_in_dim.51), calls=%async_computation.3 | async-start | bytes 262144 | tf_op jit(solution)/shard_map/all_to_all | solution.py:21
  59.5 8.6 %all-to-all-done.3 = bf16[16,512,8]{1,2,0:T(8,128)(2,1)S(1)} async-done(((bf16[16,512,8]{1,2,0:T(8,128)(2,1)}), bf16[16,512,8]{1,2,0:T(8,128)(2,1)S(1)}, u32[]{:S(2)}, u32[]{:S(2)}) %all-to-all-start.3) | async-done | bytes 131104 | tf_op jit(solution)/shard_map/all_to_all | solution.py:21
  68.2 0.2 convolution_convert_fusion.1
  68.4 0.7 reshape.61
  69.0 4.9 %all-to-all-start.4 = ((bf16[32,4,256]{2,1,0:T(4,128)(2,1)}), bf16[32,4,256]{2,1,0:T(4,128)(2,1)S(1)}, u32[]{:S(2)}, u32[]{:S(2)}) async-start(bf16[32,4,256]{2,1,0:T(4,128)(2,1)} %reshape.61), calls=%async_computation.4 | async-start | bytes 131072 | tf_op jit(solution)/shard_map/all_to_all | solution.py:15
  73.9 0.0 copy-done.1
  73.9 10.4 %fusion.1 = bf16[30720,8]{0,1:T(8,128)(2,1)S(1)} fusion(bf16[512,8]{0,1:T(8,128)(2,1)S(1)} %reduce_sum.33, s32[512]{0:T(512)S(1)} %copy-done.1), kind=kOutput, calls=%fused_computation.3 | convolution fusion | flops 267632640 | bytes 501760 | tf_op jit(solution)/shard_map/dot_general | solution.py:70
  84.3 0.6 reshape.58
  84.9 1.1 copy.11
  86.0 0.0 all-to-all-done.4
  86.0 9.8 %all-to-all-start.1 = ((bf16[32,960,8]{1,2,0:T(8,128)(2,1)}), bf16[32,960,8]{1,2,0:T(8,128)(2,1)S(1)}, u32[]{:S(2)}, u32[]{:S(2)}) async-start(bf16[32,960,8]{1,2,0:T(8,128)(2,1)} %copy.11), calls=%async_computation.1 | async-start | bytes 1048576 | tf_op jit(solution)/shard_map/all_to_all | solution.py:15
  95.8 0.1 reduce_sum.35
  95.9 17.8 %all-to-all-done.1 = bf16[32,960,8]{1,2,0:T(8,128)(2,1)S(1)} async-done(((bf16[32,960,8]{1,2,0:T(8,128)(2,1)}), bf16[32,960,8]{1,2,0:T(8,128)(2,1)S(1)}, u32[]{:S(2)}, u32[]{:S(2)}) %all-to-all-start.1) | async-done | bytes 491552 | tf_op jit(solution)/shard_map/all_to_all | solution.py:15
  113.7 0.6 broadcast_in_dim.52
  114.4 4.8 %all-to-all-start.5 = ((bf16[32,4,256]{2,1,0:T(4,128)(2,1)}), bf16[32,4,256]{2,1,0:T(4,128)(2,1)S(1)}, u32[]{:S(2)}, u32[]{:S(2)}) async-start(bf16[32,4,256]{2,1,0:T(4,128)(2,1)} %broadcast_in_dim.52), calls=%async_computation.5 | async-start | bytes 131072 | tf_op jit(solution)/shard_map/all_to_all | solution.py:21
  119.2 0.7 convert_reduce_fusion
  119.9 8.4 %all-to-all-done.5 = bf16[32,4,256]{2,1,0:T(4,128)(2,1)S(1)} async-done(((bf16[32,4,256]{2,1,0:T(4,128)(2,1)}), bf16[32,4,256]{2,1,0:T(4,128)(2,1)S(1)}, u32[]{:S(2)}, u32[]{:S(2)}) %all-to-all-start.5) | async-done | bytes 65568 | tf_op jit(solution)/shard_map/all_to_all | solution.py:21
  128.3 0.7 reshape.62
  (3 shorter events, 0.0 us)
Async XLA Ops:
  0.6 12.3 %copy-start = (bf16[512,256]{1,0:T(8,128)(2,1)S(1)}, bf16[512,256]{1,0:T(8,128)(2,1)}, u32[]{:S(2)}) copy-start(bf16[512,256]{1,0:T(8,128)(2,1)} %param.7) | copy-start | bytes 786436
  0.6 73.2 %copy-start.1 = (s32[512]{0:T(512)S(1)}, s32[512]{0:T(512)}, u32[]{:S(2)}) copy-start(s32[512]{0:T(512)} %param.4) | copy-start | bytes 6148
  2.8 27.8 %all-to-all-start.2 = ((bf16[32,960,8]{1,2,0:T(8,128)(2,1)}), bf16[32,960,8]{1,2,0:T(8,128)(2,1)S(1)}, u32[]{:S(2)}, u32[]{:S(2)}) async-start(bf16[32,960,8]{1,2,0:T(8,128)(2,1)} %broadcast_in_dim.47), calls=%async_computation.2 | async-start | bytes 1048576 | tf_op jit(solution)/shard_map/all_to_all | solution.py:21
  30.5 21.1 %all-to-all-start = ((bf16[16,512,8]{1,2,0:T(8,128)(2,1)}), bf16[16,512,8]{1,2,0:T(8,128)(2,1)S(1)}, u32[]{:S(2)}, u32[]{:S(2)}) async-start(bf16[16,512,8]{1,2,0:T(8,128)(2,1)} %fusion.3), calls=%async_computation | async-start | bytes 262144 | tf_op jit(solution)/shard_map/all_to_all | solution.py:15
  52.3 15.9 %all-to-all-start.3 = ((bf16[16,512,8]{1,2,0:T(8,128)(2,1)}), bf16[16,512,8]{1,2,0:T(8,128)(2,1)S(1)}, u32[]{:S(2)}, u32[]{:S(2)}) async-start(bf16[16,512,8]{1,2,0:T(8,128)(2,1)} %broadcast_in_dim.51), calls=%async_computation.3 | async-start | bytes 262144 | tf_op jit(solution)/shard_map/all_to_all | solution.py:21
  69.0 17.0 %all-to-all-start.4 = ((bf16[32,4,256]{2,1,0:T(4,128)(2,1)}), bf16[32,4,256]{2,1,0:T(4,128)(2,1)S(1)}, u32[]{:S(2)}, u32[]{:S(2)}) async-start(bf16[32,4,256]{2,1,0:T(4,128)(2,1)} %reshape.61), calls=%async_computation.4 | async-start | bytes 131072 | tf_op jit(solution)/shard_map/all_to_all | solution.py:15
  86.0 27.7 %all-to-all-start.1 = ((bf16[32,960,8]{1,2,0:T(8,128)(2,1)}), bf16[32,960,8]{1,2,0:T(8,128)(2,1)S(1)}, u32[]{:S(2)}, u32[]{:S(2)}) async-start(bf16[32,960,8]{1,2,0:T(8,128)(2,1)} %copy.11), calls=%async_computation.1 | async-start | bytes 1048576 | tf_op jit(solution)/shard_map/all_to_all | solution.py:15
  114.4 13.9 %all-to-all-start.5 = ((bf16[32,4,256]{2,1,0:T(4,128)(2,1)}), bf16[32,4,256]{2,1,0:T(4,128)(2,1)S(1)}, u32[]{:S(2)}, u32[]{:S(2)}) async-start(bf16[32,4,256]{2,1,0:T(4,128)(2,1)} %broadcast_in_dim.52), calls=%async_computation.5 | async-start | bytes 131072 | tf_op jit(solution)/shard_map/all_to_all | solution.py:21
where the time goes:
time: 130 us; the launch traced here: 129 us
  waiting for transfers between devices  49.4 us (38%)
  starting transfers between devices  47.3 us (36%)
  local copies, waits for them, and re-layouts  17 us (13%)
  matrix products  12.3 us (9%)
  other arithmetic  2.18 us (2%)
    all_to_all x3, waiting for transfers between devices, sent_to_all(): lax.all_to_all(jnp.broadcast_to(x[None], (peers, *x.shape)), axis, 0, 0,...  31.5 us
    all_to_all x3, starting transfers between devices, sent_and_summed(): lax.all_to_all(blocks, axis, split_axis=0, concat_axis=0, tiled=True)  25.1 us
    all_to_all x3, starting transfers between devices, sent_to_all(): lax.all_to_all(jnp.broadcast_to(x[None], (peers, *x.shape)), axis, 0, 0,...  22.2 us
    all_to_all x3, waiting for transfers between devices, sent_and_summed(): lax.all_to_all(blocks, axis, split_axis=0, concat_axis=0, tiled=True)  17.8 us
    dot_general x1, matrix products, on_device(): jnp.dot(one_hot, token_grad, preferred_element_type=jnp.float32)  10.4 us
    gather x2, local copies, waits for them, and re-layouts, lookup_rows(): picked = jnp.take(piece, jnp.clip(token_ids, 0, count - 1), axis=0)  5.37 us
    all_to_all x1, local copies, waits for them, and re-layouts, sent_to_all(): lax.all_to_all(jnp.broadcast_to(x[None], (peers, *x.shape)), axis, 0, 0,...  5.23 us
  transfers between devices with their start and end apart: 6, of which 4 were waited for; matrix products, arithmetic and copies ran while one was open for 21% of the time, Pallas kernels for 0%

commit v1 on v0

v1 whole, which is shorter than its diff:
```python
import jax
import jax.numpy as jnp
from jax import lax
from jax.experimental import pallas as pl
from jax.experimental.pallas import tpu as pltpu
from jax.sharding import PartitionSpec as P

F32, BF16, I32 = jnp.float32, jnp.bfloat16, jnp.int32
LANES = 128


def run(body, out, *args, flops, limit):
    size = lambda a: a.size * a.dtype.itemsize
    vmem = pl.BlockSpec(memory_space=pltpu.VMEM)
    return pl.pallas_call(
        body,
        out_shape=out,
        in_specs=[vmem] * len(args),
        out_specs=vmem,
        compiler_params=pltpu.CompilerParams(vmem_limit_bytes=limit * 2**20),
        cost_estimate=pl.CostEstimate(
            flops=flops, bytes_accessed=sum(map(size, args)) + size(out), transcendentals=0
        ),
    )(*args)


def exchange(blocks, axis):
    return lax.all_to_all(blocks, axis, split_axis=0, concat_axis=0, tiled=True)


def contract_last(a, b):
    return lax.dot_general(a, b, (((1,), (1,)), ((), ())), preferred_element_type=F32)


def columns_body(table, out):
    width = out.shape[1]
    first = lax.axis_index("hidden") * width
    row = lax.broadcasted_iota(I32, (width, table.shape[1]), 0)
    lane = lax.broadcasted_iota(I32, (width, table.shape[1]), 1)
    pick = (lane == row + first).astype(F32).astype(BF16)
    mine = contract_last(pick, table[...]).astype(BF16)
    for peer in range(out.shape[0]):
        out[peer] = mine


def lookup_body(owners, table, ids, out):
    width = out.shape[1]
    rows = table.shape[1]
    token = ids[...]
    owner = ((token >> 6) * 4370) >> 16
    row = token - owner * rows
    count = token.shape[1]
    hot = (lax.broadcasted_iota(I32, (rows, count), 0) == row).astype(F32).astype(BF16)
    every = jnp.dot(table[...], hot, preferred_element_type=F32)
    total = jnp.zeros((width, count), F32)
    for v in range(owners):
        total = jnp.where(owner == v, every[v * width : (v + 1) * width], total)
    mine = total.astype(BF16)
    for peer in range(out.shape[0]):
        out[peer] = mine


def token_grad_body(partials, ids, out):
    total = partials[0].astype(F32)
    for peer in range(1, partials.shape[0]):
        total = total + partials[peer].astype(F32)
    count = total.shape[1]
    token = ids[...]
    digits = jnp.concatenate([token >> 7, token & 127], axis=0).astype(F32)
    packed = jnp.concatenate([total.astype(BF16), digits.astype(BF16)], axis=1)
    for peer in range(out.shape[0]):
        out[peer] = packed


def segments_body(arrived, out):
    sources, width, _ = arrived.shape
    rows = out.shape[1]
    count = arrived.shape[2] - LANES
    chunks = count // LANES
    groups = -(-rows // LANES)
    first = lax.axis_index("vocab") * rows

    def step(source, total):
        block = arrived[source]
        grad = block[:, :count].astype(F32)
        digits = block[:, count:].astype(F32).astype(I32)
        row = digits[:chunks] * LANES + digits[chunks:] - first
        high, low = row >> 7, row & 127
        left, right = [], []
        for c in range(chunks):
            at = slice(c * LANES, (c + 1) * LANES)
            high_c = jnp.broadcast_to(high[c : c + 1], (width, LANES))
            low_c = jnp.broadcast_to(low[c : c + 1], (LANES, LANES))
            part = grad[:, at]
            left.append(
                jnp.concatenate([jnp.where(high_c == g, part, 0.0) for g in range(groups)], axis=0).astype(BF16)
            )
            right.append(
                (lax.broadcasted_iota(I32, (LANES, LANES), 0) == low_c).astype(F32).astype(BF16)
            )
        return total + contract_last(jnp.concatenate(left, axis=1), jnp.concatenate(right, axis=1))

    total = lax.fori_loop(0, sources, step, jnp.zeros((groups * width, LANES), F32), unroll=4)
    for g in range(groups):
        wide = min(LANES, rows - g * LANES)
        out[:, g * LANES : g * LANES + wide] = total[g * width : (g + 1) * width, :wide]


def projection_body(embedded, grad_out, out):
    result = jnp.dot(embedded[...], grad_out[...], preferred_element_type=F32)
    across = result.shape[1] // LANES
    for piece in range(out.shape[0]):
        i, j = piece // across, piece % across
        out[piece] = result[i * 8 : i * 8 + 8, j * LANES : (j + 1) * LANES].astype(BF16)


def sum_body(arrived, out):
    total = arrived[0].astype(F32)
    for peer in range(1, arrived.shape[0]):
        total = total + arrived[peer].astype(F32)
    mine = total.astype(BF16)
    for peer in range(out.shape[0]):
        out[peer] = mine


def assemble_body(arrived, out):
    across = out.shape[1] // LANES
    for piece in range(arrived.shape[0]):
        i, j = piece // across, piece % across
        out[i * 8 : i * 8 + 8, j * LANES : (j + 1) * LANES] = arrived[piece].astype(F32)


def on_device(token_ids, table, projection, grad_out):
    owners, peers = lax.axis_size("vocab"), lax.axis_size("hidden")
    rows, depth = table.shape
    width = depth // peers
    count = token_ids.shape[0]
    hidden = projection.shape[1]
    S = jax.ShapeDtypeStruct

    columns = run(columns_body, S((owners, width, rows), BF16), table, flops=2 * depth * rows * width, limit=4)
    columns = exchange(columns, "vocab")

    partial_grad = contract_last(projection, grad_out).astype(BF16).reshape(peers, width, count)
    partial_grad = exchange(partial_grad, "hidden")

    def lookup(table, ids, out):
        lookup_body(owners, table, ids, out)

    looked = run(
        lookup,
        S((peers, width, count), BF16),
        columns.reshape(owners * width, rows),
        token_ids.reshape(1, count),
        flops=2 * owners * width * rows * count,
        limit=8,
    )
    embedded = exchange(looked, "hidden").reshape(depth, count)

    packed = run(
        token_grad_body,
        S((owners, width, count + LANES), BF16),
        partial_grad,
        token_ids.reshape(count // LANES, LANES),
        flops=peers * width * count,
        limit=4,
    )
    packed = exchange(packed, "vocab")

    pieces = run(
        projection_body,
        S((owners, 8, depth * hidden // owners // 8), BF16),
        embedded,
        grad_out,
        flops=2 * depth * count * hidden,
        limit=4,
    )
    pieces = exchange(pieces, "vocab")
    summed = run(sum_body, S(pieces.shape, BF16), pieces, flops=pieces.size, limit=4)
    summed = exchange(summed, "vocab")
    table_grad = run(
        segments_body,
        S((width, rows), F32),
        packed,
        flops=2 * owners * count * width * 8 * LANES,
        limit=8,
    )
    projection_grad = run(assemble_body, S((depth, hidden), F32), summed, flops=summed.size, limit=4)
    return table_grad.T, projection_grad


def solution(mesh):
    placed = (P("vocab"), P("vocab", None), P(None, "hidden"), P("vocab", "hidden"))
    return jax.shard_map(
        on_device,
        mesh=mesh,
        in_specs=placed,
        out_specs=(P("vocab", "hidden"), P(None, "hidden")),
        check_vma=False,
    )
```

time: 130 us -> 110 us (0.85)
  blocking collectives: 0 us -> 27.6 us
  starting transfers between devices: 47.3 us -> 28.3 us
  local copies, waits for them, and re-layouts: 17 us -> 1.66 us
  matrix products: 12.3 us -> 0.88 us
  Pallas kernels: 0 us -> 7.34 us
  waiting for transfers between devices: 49.4 us -> 42.8 us
  other arithmetic: 2.18 us -> 0 us
    all_to_all x0 -> x1, blocking collectives: none -> 27.6 us  [exchange(): return lax.all_to_all(blocks, axis, split_axis=0, concat_axis=0, tiled=True)]
    all_to_all x6 -> x5, starting transfers between devices: 47.3 us -> 28.3 us  [exchange(): return lax.all_to_all(blocks, axis, split_axis=0, concat_axis=0, tiled=True)]
    dot_general x3 -> x1, matrix products: 12.3 us -> 0.88 us  [contract_last(): lax.dot_general(a, b, (((1,), (1,)), ((), ())), preferred_element_type=F32)]
    pallas_call x0 -> x7, Pallas kernels: none -> 7.34 us  [run(): pl.pallas_call(body, out_shape=out, in_specs=[vmem] * len(args), out_spec...]
    all_to_all x6 -> x5, waiting for transfers between devices: 49.4 us -> 42.8 us  [exchange(): return lax.all_to_all(blocks, axis, split_axis=0, concat_axis=0, tiled=True)]
    gather x2 -> x0, local copies, waits for them, and re-layouts: 5.37 us -> none  [lookup_rows(): picked = jnp.take(piece, jnp.clip(token_ids, 0, count - 1), axis=0)]
    all_to_all x1 -> x0, local copies, waits for them, and re-layouts: 5.23 us -> none  [sent_to_all(): lax.all_to_all(jnp.broadcast_to(x[None], (peers, *x.shape)), axis, 0, 0,...]
    reshape x3 -> x0, local copies, waits for them, and re-layouts: 2.37 us -> none  [cut_along(): x.reshape(*lengths[:dim], peers, lengths[dim] // peers, *lengths[dim + 1:])]
  transfers between devices with their start and end apart: 6 -> 5, of which waited for: 4 -> 5; matrix products, arithmetic and copies ran while one was open for 21% -> 1% of each run, Pallas kernels for 0% -> 5%
where the time goes in v1:
time: 110 us; the launch traced here: 109 us
  waiting for transfers between devices  42.8 us (39%)
  starting transfers between devices  28.3 us (26%)
  blocking collectives  27.6 us (25%)
  Pallas kernels  7.34 us (7%)
  local copies, waits for them, and re-layouts  1.66 us (2%)
    all_to_all x5, waiting for transfers between devices, exchange(): return lax.all_to_all(blocks, axis, split_axis=0, concat_axis=0, tiled=True)  42.8 us
    all_to_all x5, starting transfers between devices, exchange(): return lax.all_to_all(blocks, axis, split_axis=0, concat_axis=0, tiled=True)  28.3 us
    all_to_all x1, blocking collectives, exchange(): return lax.all_to_all(blocks, axis, split_axis=0, concat_axis=0, tiled=True)  27.6 us
    pallas_call x7, Pallas kernels, run(): pl.pallas_call(body, out_shape=out, in_specs=[vmem] * len(args), out_spec...  7.34 us
  transfers between devices with their start and end apart: 5, of which 5 were waited for; matrix products, arithmetic and copies ran while one was open for 1% of the time, Pallas kernels for 5%

profile of v1, /device:TPU:8, one launch (start us, length us, event | category | flops | bytes accessed | tf_op | source)
XLA Modules:
  0.0 109.2 jit_solution(12811999531778747799)
XLA Ops:
  0.6 0.0 copy-start
  0.6 0.0 copy-start.2
  0.7 1.0 copy-done.2
  1.6 0.2 shard_map.61
  1.8 27.6 %all_to_all.30 = bf16[32,8,960]{2,1,0:T(8,128)(2,1)S(1)} all-to-all(bf16[32,8,960]{2,1,0:T(8,128)(2,1)S(1)} %shard_map.61), channel_id=1, replica_groups=mesh['vocab'=32,'hidden'=16] {'vocab'}, dimensions={0} | all-to-all | bytes 983040 | tf_op jit(solution)/shard_map/all_to_all | solution.py:28
  29.4 0.0 copy-start.3
  29.4 0.7 copy-done.3
  30.1 1.1 %shard_map.62 = bf16[16,8,512]{2,1,0:T(8,128)(2,1)} custom-call(bf16[256,960]{1,0:T(8,128)(2,1)S(1)} %bitcast.10, s32[1,512]{1,0:T(1,128)S(1)} %bitcast.11), custom_call_target="tpu_custom_call" | custom-call | flops 251658240 | bytes 624640 | tf_op jit(solution)/shard_map/pallas_call | solution.py:15
  31.2 0.0 copy-start.1
  31.2 10.6 %all-to-all-start.3 = ((bf16[16,8,512]{2,1,0:T(8,128)(2,1)}), bf16[16,8,512]{2,1,0:T(8,128)(2,1)S(1)}, u32[]{:S(2)}, u32[]{:S(2)}) async-start(bf16[16,8,512]{2,1,0:T(8,128)(2,1)} %shard_map.62), calls=%async_computation.3 | async-start | bytes 262144 | tf_op jit(solution)/shard_map/all_to_all | solution.py:28
  41.8 0.0 copy-done
  41.8 0.0 copy-done.1
  41.8 0.9 fusion
  42.7 7.7 %all-to-all-done.3 = bf16[16,8,512]{2,1,0:T(8,128)(2,1)S(1)} async-done(((bf16[16,8,512]{2,1,0:T(8,128)(2,1)}), bf16[16,8,512]{2,1,0:T(8,128)(2,1)S(1)}, u32[]{:S(2)}, u32[]{:S(2)}) %all-to-all-start.3) | async-done | bytes 131104 | tf_op jit(solution)/shard_map/all_to_all | solution.py:28
  50.4 3.5 %all-to-all-start = ((bf16[16,8,512]{2,1,0:T(8,128)(2,1)}), bf16[16,8,512]{2,1,0:T(8,128)(2,1)S(1)}, u32[]{:S(2)}, u32[]{:S(2)}) async-start(bf16[16,8,512]{2,1,0:T(8,128)(2,1)} %fusion), calls=%async_computation | async-start | bytes 262144 | tf_op jit(solution)/shard_map/all_to_all | solution.py:28
  53.9 0.8 shard_map.63
  54.8 7.8 %all-to-all-done.partials = bf16[16,8,512]{2,1,0:T(8,128)(2,1)S(1)} async-done(((bf16[16,8,512]{2,1,0:T(8,128)(2,1)}), bf16[16,8,512]{2,1,0:T(8,128)(2,1)S(1)}, u32[]{:S(2)}, u32[]{:S(2)}) %all-to-all-start) | async-done | bytes 131104 | tf_op jit(solution)/shard_map/all_to_all | solution.py:28
  62.6 4.9 %all-to-all-start.4 = ((bf16[32,8,128]{2,1,0:T(8,128)(2,1)}), bf16[32,8,128]{2,1,0:T(8,128)(2,1)S(1)}, u32[]{:S(2)}, u32[]{:S(2)}) async-start(bf16[32,8,128]{2,1,0:T(8,128)(2,1)} %shard_map.63), calls=%async_computation.4 | async-start | bytes 131072 | tf_op jit(solution)/shard_map/all_to_all | solution.py:28
  67.4 0.8 shard_map.59
  68.2 8.6 %all-to-all-done.4.arrived = bf16[32,8,128]{2,1,0:T(8,128)(2,1)S(1)} async-done(((bf16[32,8,128]{2,1,0:T(8,128)(2,1)}), bf16[32,8,128]{2,1,0:T(8,128)(2,1)S(1)}, u32[]{:S(2)}, u32[]{:S(2)}) %all-to-all-start.4) | async-done | bytes 65568 | tf_op jit(solution)/shard_map/all_to_all | solution.py:28
  76.8 4.7 %all-to-all-start.1 = ((bf16[32,8,640]{2,1,0:T(8,128)(2,1)}), bf16[32,8,640]{2,1,0:T(8,128)(2,1)S(1)}, u32[]{:S(2)}, u32[]{:S(2)}) async-start(bf16[32,8,640]{2,1,0:T(8,128)(2,1)} %shard_map.59), calls=%async_computation.1 | async-start | bytes 655360 | tf_op jit(solution)/shard_map/all_to_all | solution.py:28
  81.5 0.7 shard_map.64
  82.2 12.6 %all-to-all-done.1.arrived = bf16[32,8,640]{2,1,0:T(8,128)(2,1)S(1)} async-done(((bf16[32,8,640]{2,1,0:T(8,128)(2,1)}), bf16[32,8,640]{2,1,0:T(8,128)(2,1)S(1)}, u32[]{:S(2)}, u32[]{:S(2)}) %all-to-all-start.1) | async-done | bytes 327712 | tf_op jit(solution)/shard_map/all_to_all | solution.py:28
  94.8 4.7 %all-to-all-start.5 = ((bf16[32,8,128]{2,1,0:T(8,128)(2,1)}), bf16[32,8,128]{2,1,0:T(8,128)(2,1)S(1)}, u32[]{:S(2)}, u32[]{:S(2)}) async-start(bf16[32,8,128]{2,1,0:T(8,128)(2,1)} %shard_map.64), calls=%async_computation.5 | async-start | bytes 131072 | tf_op jit(solution)/shard_map/all_to_all | solution.py:28
  99.5 3.1 %shard_map.60 = f32[8,960]{1,0:T(8,128)} custom-call(bf16[32,8,640]{2,1,0:T(8,128)(2,1)S(1)} %all-to-all-done.1.arrived), custom_call_target="tpu_custom_call" | custom-call | flops 268435456 | bytes 358400 | tf_op jit(solution)/shard_map/pallas_call | solution.py:15
  102.6 6.0 %all-to-all-done.5.arrived = bf16[32,8,128]{2,1,0:T(8,128)(2,1)S(1)} async-done(((bf16[32,8,128]{2,1,0:T(8,128)(2,1)}), bf16[32,8,128]{2,1,0:T(8,128)(2,1)S(1)}, u32[]{:S(2)}, u32[]{:S(2)}) %all-to-all-start.5) | async-done | bytes 65568 | tf_op jit(solution)/shard_map/all_to_all | solution.py:28
  108.6 0.7 shard_map.65
Async XLA Ops:
  0.6 41.1 %copy-start = (bf16[128,256]{1,0:T(8,128)(2,1)S(1)}, bf16[128,256]{1,0:T(8,128)(2,1)}, u32[]{:S(2)}) copy-start(bf16[128,256]{1,0:T(8,128)(2,1)} %param.6) | copy-start | bytes 196612
  0.6 1.0 copy-start.2
  29.4 0.7 copy-start.3
  31.2 10.6 %copy-start.1 = (bf16[512,256]{1,0:T(8,128)(2,1)S(1)}, bf16[512,256]{1,0:T(8,128)(2,1)}, u32[]{:S(2)}) copy-start(bf16[512,256]{1,0:T(8,128)(2,1)} %grad_out.1) | copy-start | bytes 786436
  31.2 19.2 %all-to-all-start.3 = ((bf16[16,8,512]{2,1,0:T(8,128)(2,1)}), bf16[16,8,512]{2,1,0:T(8,128)(2,1)S(1)}, u32[]{:S(2)}, u32[]{:S(2)}) async-start(bf16[16,8,512]{2,1,0:T(8,128)(2,1)} %shard_map.62), calls=%async_computation.3 | async-start | bytes 262144 | tf_op jit(solution)/shard_map/all_to_all | solution.py:28
  50.4 12.1 %all-to-all-start = ((bf16[16,8,512]{2,1,0:T(8,128)(2,1)}), bf16[16,8,512]{2,1,0:T(8,128)(2,1)S(1)}, u32[]{:S(2)}, u32[]{:S(2)}) async-start(bf16[16,8,512]{2,1,0:T(8,128)(2,1)} %fusion), calls=%async_computation | async-start | bytes 262144 | tf_op jit(solution)/shard_map/all_to_all | solution.py:28
  62.6 14.3 %all-to-all-start.4 = ((bf16[32,8,128]{2,1,0:T(8,128)(2,1)}), bf16[32,8,128]{2,1,0:T(8,128)(2,1)S(1)}, u32[]{:S(2)}, u32[]{:S(2)}) async-start(bf16[32,8,128]{2,1,0:T(8,128)(2,1)} %shard_map.63), calls=%async_computation.4 | async-start | bytes 131072 | tf_op jit(solution)/shard_map/all_to_all | solution.py:28
  76.8 17.9 %all-to-all-start.1 = ((bf16[32,8,640]{2,1,0:T(8,128)(2,1)}), bf16[32,8,640]{2,1,0:T(8,128)(2,1)S(1)}, u32[]{:S(2)}, u32[]{:S(2)}) async-start(bf16[32,8,640]{2,1,0:T(8,128)(2,1)} %shard_map.59), calls=%async_computation.1 | async-start | bytes 655360 | tf_op jit(solution)/shard_map/all_to_all | solution.py:28
  94.8 13.8 %all-to-all-start.5 = ((bf16[32,8,128]{2,1,0:T(8,128)(2,1)}), bf16[32,8,128]{2,1,0:T(8,128)(2,1)S(1)}, u32[]{:S(2)}, u32[]{:S(2)}) async-start(bf16[32,8,128]{2,1,0:T(8,128)(2,1)} %shard_map.64), calls=%async_computation.5 | async-start | bytes 131072 | tf_op jit(solution)/shard_map/all_to_all | solution.py:28

commit v2 on v1

v2 whole, which is shorter than its diff:
```python
import jax
import jax.numpy as jnp
from jax import lax
from jax.experimental import pallas as pl
from jax.experimental.pallas import tpu as pltpu
from jax.sharding import PartitionSpec as P

F32, BF16, I32 = jnp.float32, jnp.bfloat16, jnp.int32
LANES, SUBLANES = 128, 8
NEAR = 8


def run(body, out, *args, flops, limit):
    size = lambda a: a.size * a.dtype.itemsize
    vmem = pl.BlockSpec(memory_space=pltpu.VMEM)
    outs = jax.tree.leaves(out)
    return pl.pallas_call(
        body,
        out_shape=out,
        in_specs=[vmem] * len(args),
        out_specs=jax.tree.map(lambda _: vmem, out),
        compiler_params=pltpu.CompilerParams(vmem_limit_bytes=limit * 2**20),
        cost_estimate=pl.CostEstimate(
            flops=flops, bytes_accessed=sum(map(size, [*args, *outs])), transcendentals=0
        ),
    )(*args)


def exchange(blocks, axis, groups=None):
    return lax.all_to_all(blocks, axis, split_axis=0, concat_axis=0, tiled=True, axis_index_groups=groups)


def contract_last(a, b):
    return lax.dot_general(a, b, (((1,), (1,)), ((), ())), preferred_element_type=F32)


def one_hot_rows(which, rows):
    shape = (rows, which.shape[1])
    return (lax.broadcasted_iota(I32, shape, 0) == which).astype(F32).astype(BF16)


def owner_and_row(token, rows):
    owner = ((token >> 6) * 4370) >> 16
    return owner, token - owner * rows


def columns_body(table, out):
    width = out.shape[1]
    first = lax.axis_index("hidden") * width
    shape = (width, table.shape[1])
    lane = lax.broadcasted_iota(I32, shape, 1)
    pick = (lane == lax.broadcasted_iota(I32, shape, 0) + first).astype(F32).astype(BF16)
    mine = contract_last(pick, table[...]).astype(BF16)
    for peer in range(out.shape[0]):
        out[peer] = mine


def lookup_body(owners, table, ids, partials, out):
    width = partials.shape[1]
    count = ids.shape[1]
    owner, row = owner_and_row(ids[...], table.shape[1])
    every = jnp.dot(table[...], one_hot_rows(row, table.shape[1]), preferred_element_type=F32)
    total = jnp.zeros((width, count), F32)
    for v in range(owners):
        total = jnp.where(owner == v, every[v * width : (v + 1) * width], total)
    mine = total.astype(BF16)
    for peer in range(out.shape[0]):
        out[peer, :width] = mine
        out[peer, width:] = partials[peer]


def products_body(rows, arrived, grad_out, ids, out):
    peers = arrived.shape[0]
    width = arrived.shape[1] // 2
    embedded = jnp.concatenate([arrived[p, :width] for p in range(peers)], axis=0)
    product = jnp.dot(embedded, grad_out[...], preferred_element_type=F32).astype(BF16)
    grad = arrived[0, width:].astype(F32)
    for peer in range(1, peers):
        grad = grad + arrived[peer, width:].astype(F32)
    owner, row = owner_and_row(ids[...], rows)
    digits = jnp.concatenate([owner * 8 + (row >> 7), row & 127], axis=0).astype(F32)
    depth = product.shape[0]
    across = product.shape[1] // LANES
    chunks = grad.shape[1] // LANES
    blocks = [product[:, j * LANES : (j + 1) * LANES] for j in range(across)]
    small = [grad[:, c * LANES : (c + 1) * LANES].astype(BF16) for c in range(chunks)] + [digits.astype(BF16)]
    for peer in range(out.shape[0]):
        for j in range(across):
            out[peer, j * depth : (j + 1) * depth] = blocks[j]
        for c in range(chunks + 1):
            at = across * depth + c * SUBLANES
            out[peer, at : at + SUBLANES] = small[c]


def near_sums_body(product_rows, arrived, out):
    near = arrived.shape[0]
    far = out.shape[0]
    chunks = (arrived.shape[1] - product_rows) // SUBLANES - 1
    y = lax.axis_index("vocab") & (NEAR - 1)

    total = arrived[0, :product_rows].astype(F32)
    for peer in range(1, near):
        total = total + arrived[peer, :product_rows].astype(F32)
    total = total.astype(BF16)
    for peer in range(far):
        out[peer, :product_rows] = total

    sums = jnp.zeros((far * 8 * SUBLANES, LANES), F32)
    for peer in range(near):
        at = product_rows + chunks * SUBLANES
        digits = arrived[peer, at : at + SUBLANES].astype(F32).astype(I32)
        high, low = digits[:chunks], digits[chunks:]
        mine = ((high >> 3) & (NEAR - 1)) == y
        group = jnp.where(mine, (high >> 6) * 8 + (high & 7), -1)
        left, right = [], []
        for c in range(chunks):
            start = product_rows + c * SUBLANES
            part = arrived[peer, start : start + SUBLANES].astype(F32)
            group_c = jnp.broadcast_to(group[c : c + 1], part.shape)
            left.append(
                jnp.concatenate([jnp.where(group_c == g, part, 0.0) for g in range(far * 8)], axis=0).astype(BF16)
            )
            right.append(one_hot_rows(low[c : c + 1], LANES))
        sums = sums + contract_last(jnp.concatenate(left, axis=1), jnp.concatenate(right, axis=1))
    sums = sums.astype(BF16)
    for peer in range(far):
        out[peer, product_rows:] = sums[peer * 8 * SUBLANES : (peer + 1) * 8 * SUBLANES]


def far_sums_body(product_rows, arrived, table_grad, projection_grad):
    total = arrived[0].astype(F32)
    for peer in range(1, arrived.shape[0]):
        total = total + arrived[peer].astype(F32)
    depth = projection_grad.shape[0]
    for j in range(projection_grad.shape[1] // LANES):
        projection_grad[:, j * LANES : (j + 1) * LANES] = total[j * depth : (j + 1) * depth]
    rows = table_grad.shape[1]
    for g in range(-(-rows // LANES)):
        at = product_rows + g * SUBLANES
        wide = min(LANES, rows - g * LANES)
        table_grad[:, g * LANES : g * LANES + wide] = total[at : at + SUBLANES, :wide]


def on_device(token_ids, table, projection, grad_out):
    owners, peers = lax.axis_size("vocab"), lax.axis_size("hidden")
    near, far = NEAR, owners // NEAR
    same_x = [[x * near + y for y in range(near)] for x in range(far)]
    same_y = [[x * near + y for x in range(far)] for y in range(near)]
    rows, depth = table.shape
    width = depth // peers
    count = token_ids.shape[0]
    hidden = projection.shape[1]
    product_rows = depth * hidden // LANES
    chunks = count // LANES
    S = jax.ShapeDtypeStruct

    columns = run(columns_body, S((owners, width, rows), BF16), table, flops=2 * depth * rows * width, limit=4)
    columns = exchange(columns, "vocab").reshape(owners * width, rows)

    partials = contract_last(projection, grad_out).astype(BF16).reshape(peers, width, count)

    def lookup(*refs):
        lookup_body(owners, *refs)

    def products(*refs):
        products_body(rows, *refs)

    def near_sums(*refs):
        near_sums_body(product_rows, *refs)

    def far_sums(*refs):
        far_sums_body(product_rows, *refs)

    looked = run(
        lookup,
        S((peers, 2 * width, count), BF16),
        columns,
        token_ids.reshape(1, count),
        partials,
        flops=2 * owners * width * rows * count,
        limit=8,
    )
    looked = exchange(looked, "hidden")

    made = run(
        products,
        S((near, product_rows + (chunks + 1) * SUBLANES, LANES), BF16),
        looked,
        grad_out,
        token_ids.reshape(chunks, LANES),
        flops=2 * depth * count * hidden,
        limit=8,
    )
    made = exchange(made, "vocab", same_x)

    summed = run(
        near_sums,
        S((far, product_rows + 8 * SUBLANES, LANES), BF16),
        made,
        flops=2 * near * count * far * 8 * SUBLANES * LANES,
        limit=8,
    )
    summed = exchange(summed, "vocab", same_y)

    table_grad, projection_grad = run(
        far_sums, (S((width, rows), F32), S((depth, hidden), F32)), summed, flops=summed.size, limit=8
    )
    return table_grad.T, projection_grad


def solution(mesh):
    placed = (P("vocab"), P("vocab", None), P(None, "hidden"), P("vocab", "hidden"))
    return jax.shard_map(
        on_device,
        mesh=mesh,
        in_specs=placed,
        out_specs=(P("vocab", "hidden"), P(None, "hidden")),
        check_vma=False,
    )
```

time: 110 us -> 88.1 us (0.80)
  the two profiles are of different devices: /device:TPU:8 before, /device:TPU:1 now
where the time goes in v2:
time: 88.1 us; the launch traced here: 87.7 us
  blocking collectives  57.9 us (66%)
  waiting for transfers between devices  14.3 us (16%)
  starting transfers between devices  10.6 us (12%)
  Pallas kernels  3.08 us (3%)
  local copies, waits for them, and re-layouts  0.99 us (1%)
    all_to_all x3, blocking collectives, exchange(): lax.all_to_all(blocks, axis, split_axis=0, concat_axis=0, tiled=True, axi...  57.9 us
    all_to_all x1, waiting for transfers between devices, exchange(): lax.all_to_all(blocks, axis, split_axis=0, concat_axis=0, tiled=True, axi...  14.3 us
    all_to_all x1, starting transfers between devices, exchange(): lax.all_to_all(blocks, axis, split_axis=0, concat_axis=0, tiled=True, axi...  10.6 us
    pallas_call x5, Pallas kernels, run(): pl.pallas_call(body, out_shape=out, in_specs=[vmem] * len(args), out_spec...  3.08 us
  transfers between devices with their start and end apart: 1, of which 1 were waited for; matrix products, arithmetic and copies ran while one was open for 0% of the time, Pallas kernels for 0%

profile of v2, /device:TPU:1, one launch (start us, length us, event | category | flops | bytes accessed | tf_op | source)
XLA Modules:
  0.0 87.7 jit_solution(18079567017909775357)
XLA Ops:
  0.6 0.0 copy-start
  0.6 0.0 copy-start.2
  0.7 1.0 %copy-done.2 = bf16[960,128]{1,0:T(8,128)(2,1)S(1)} copy-done((bf16[960,128]{1,0:T(8,128)(2,1)S(1)}, bf16[960,128]{1,0:T(8,128)(2,1)}, u32[]{:S(2)}) %copy-start.2) | copy-done | bytes 245784
  1.6 1.0 %shard_map.59 = bf16[32,8,960]{2,1,0:T(8,128)(2,1)} custom-call(bf16[960,128]{1,0:T(8,128)(2,1)S(1)} %copy-done.2), custom_call_target="tpu_custom_call" | custom-call | flops 1966080 | bytes 737280 | tf_op jit(solution)/shard_map/pallas_call | solution.py:17
  2.6 0.0 copy-start.1
  2.6 10.6 %all-to-all-start = ((bf16[32,8,960]{2,1,0:T(8,128)(2,1)}), bf16[32,8,960]{2,1,0:T(8,128)(2,1)S(1)}, u32[]{:S(2)}, u32[]{:S(2)}) async-start(bf16[32,8,960]{2,1,0:T(8,128)(2,1)} %shard_map.59), calls=%async_computation | async-start | bytes 1048576 | tf_op jit(solution)/shard_map/all_to_all | solution.py:30
  13.3 0.0 copy-done
  13.3 0.0 copy-done.1
  13.3 0.2 fusion.refs_2_
  13.5 0.0 copy-start.3
  13.5 14.3 %all-to-all-done = bf16[32,8,960]{2,1,0:T(8,128)(2,1)S(1)} async-done(((bf16[32,8,960]{2,1,0:T(8,128)(2,1)}), bf16[32,8,960]{2,1,0:T(8,128)(2,1)S(1)}, u32[]{:S(2)}, u32[]{:S(2)}) %all-to-all-start) | async-done | bytes 491552 | tf_op jit(solution)/shard_map/all_to_all | solution.py:30
  27.8 0.0 copy-done.3
  27.8 0.5 shard_map.60
  28.3 24.8 %all_to_all.20.refs_0_ = bf16[16,16,512]{2,1,0:T(8,128)(2,1)S(1)} all-to-all(bf16[16,16,512]{2,1,0:T(8,128)(2,1)S(1)} %shard_map.60), channel_id=1, replica_groups=mesh['vocab'=32,'hidden'=16] {'hidden'}, dimensions={0} | all-to-all | bytes 524288 | tf_op jit(solution)/shard_map/all_to_all | solution.py:30
  53.1 0.2 shard_map.61
  53.3 23.9 %all_to_all.21.refs_0_ = bf16[8,296,128]{2,1,0:T(8,128)(2,1)S(1)} all-to-all(bf16[8,296,128]{2,1,0:T(8,128)(2,1)S(1)} %shard_map.61), channel_id=1, replica_groups={{0,16,32,48,64,80,96,112},{128,144,160,176,192,208,224,240},{256,272,28..., dimensions={0} | all-to-all | bytes 1212416 | tf_op jit(solution)/shard_map/all_to_all | solution.py:30
  77.2 0.7 shard_map.62
  77.9 9.2 %all_to_all.22.refs_0_ = bf16[4,320,128]{2,1,0:T(8,128)(2,1)S(1)} all-to-all(bf16[4,320,128]{2,1,0:T(8,128)(2,1)S(1)} %shard_map.62), channel_id=1, replica_groups={{0,128,256,384},{16,144,272,400},{32,160,288,416},{48,176,304,432},{64,..., dimensions={0} | all-to-all | bytes 655360 | tf_op jit(solution)/shard_map/all_to_all | solution.py:30
  87.1 0.7 shard_map.63
Async XLA Ops:
  0.6 12.6 %copy-start = (bf16[128,256]{1,0:T(8,128)(2,1)S(1)}, bf16[128,256]{1,0:T(8,128)(2,1)}, u32[]{:S(2)}) copy-start(bf16[128,256]{1,0:T(8,128)(2,1)} %param.6) | copy-start | bytes 196612
  0.6 1.0 %copy-start.2 = (bf16[960,128]{1,0:T(8,128)(2,1)S(1)}, bf16[960,128]{1,0:T(8,128)(2,1)}, u32[]{:S(2)}) copy-start(bf16[960,128]{1,0:T(8,128)(2,1)} %table.1) | copy-start | bytes 737284
  2.6 10.6 %copy-start.1 = (bf16[512,256]{1,0:T(8,128)(2,1)S(1)}, bf16[512,256]{1,0:T(8,128)(2,1)}, u32[]{:S(2)}) copy-start(bf16[512,256]{1,0:T(8,128)(2,1)} %refs_1_.1) | copy-start | bytes 786436
  2.6 25.2 %all-to-all-start = ((bf16[32,8,960]{2,1,0:T(8,128)(2,1)}), bf16[32,8,960]{2,1,0:T(8,128)(2,1)S(1)}, u32[]{:S(2)}, u32[]{:S(2)}) async-start(bf16[32,8,960]{2,1,0:T(8,128)(2,1)} %shard_map.59), calls=%async_computation | async-start | bytes 1048576 | tf_op jit(solution)/shard_map/all_to_all | solution.py:30
  13.5 14.3 %copy-start.3 = (s32[512]{0:T(512)S(1)}, s32[512]{0:T(512)}, u32[]{:S(2)}) copy-start(s32[512]{0:T(512)} %param.4) | copy-start | bytes 6148

commit v3 on v2

--- a/solution.py
+++ b/solution.py
@@ -55,9 +55,10 @@
         out[peer] = mine
 
 
-def lookup_body(owners, table, ids, partials, out):
-    width = partials.shape[1]
+def lookup_body(owners, table, ids, projection, grad_out, out):
+    width = out.shape[1] // 2
     count = ids.shape[1]
+    partial = contract_last(projection[...], grad_out[...])
     owner, row = owner_and_row(ids[...], table.shape[1])
     every = jnp.dot(table[...], one_hot_rows(row, table.shape[1]), preferred_element_type=F32)
     total = jnp.zeros((width, count), F32)
@@ -66,7 +67,7 @@
     mine = total.astype(BF16)
     for peer in range(out.shape[0]):
         out[peer, :width] = mine
-        out[peer, width:] = partials[peer]
+        out[peer, width:] = partial[peer * width : (peer + 1) * width].astype(BF16)
 
 
 def products_body(rows, arrived, grad_out, ids, out):
@@ -157,8 +158,6 @@
     columns = run(columns_body, S((owners, width, rows), BF16), table, flops=2 * depth * rows * width, limit=4)
     columns = exchange(columns, "vocab").reshape(owners * width, rows)
 
-    partials = contract_last(projection, grad_out).astype(BF16).reshape(peers, width, count)
-
     def lookup(*refs):
         lookup_body(owners, *refs)
 
@@ -176,8 +175,9 @@
         S((peers, 2 * width, count), BF16),
         columns,
         token_ids.reshape(1, count),
-        partials,
-        flops=2 * owners * width * rows * count,
+        projection,
+        grad_out,
+        flops=2 * owners * width * rows * count + 2 * depth * count * hidden,
         limit=8,
     )
     looked = exchange(looked, "hidden")

time: 88.1 us -> 87.8 us (level)
  blocking collectives: 57.9 us -> 82.8 us
  waiting for transfers between devices: 14.3 us -> 0 us
  starting transfers between devices: 10.6 us -> 0 us
    all_to_all x3 -> x4, blocking collectives: 57.9 us -> 82.8 us  [exchange(): lax.all_to_all(blocks, axis, split_axis=0, concat_axis=0, tiled=True, axi...]
    all_to_all x1 -> x0, waiting for transfers between devices: 14.3 us -> none  [exchange(): lax.all_to_all(blocks, axis, split_axis=0, concat_axis=0, tiled=True, axi...]
    all_to_all x1 -> x0, starting transfers between devices: 10.6 us -> none  [exchange(): lax.all_to_all(blocks, axis, split_axis=0, concat_axis=0, tiled=True, axi...]
  transfers between devices with their start and end apart: 1 -> 0, of which waited for: 1 -> 0; matrix products, arithmetic and copies ran while one was open for 0% -> 0% of each run, Pallas kernels for 0% -> 0%
where the time goes in v3:
time: 87.8 us; the launch traced here: 87.5 us
  blocking collectives  82.8 us (94%)
  Pallas kernels  2.37 us (3%)
  local copies, waits for them, and re-layouts  1.63 us (2%)
    all_to_all x4, blocking collectives, exchange(): lax.all_to_all(blocks, axis, split_axis=0, concat_axis=0, tiled=True, axi...  82.8 us
    pallas_call x5, Pallas kernels, run(): pl.pallas_call(body, out_shape=out, in_specs=[vmem] * len(args), out_spec...  2.37 us

profile of v3, /device:TPU:1, one launch (start us, length us, event | category | flops | bytes accessed | tf_op | source)
XLA Modules:
  0.0 87.5 jit_solution(4907181939759295126)
XLA Ops:
  0.6 0.0 copy-start.1
  0.6 0.9 %copy-done.1 = bf16[960,128]{1,0:T(8,128)(2,1)S(1)} copy-done((bf16[960,128]{1,0:T(8,128)(2,1)S(1)}, bf16[960,128]{1,0:T(8,128)(2,1)}, u32[]{:S(2)}) %copy-start.1) | copy-done | bytes 245784
  1.6 0.2 shard_map.59
  1.8 0.0 copy-start
  1.8 0.0 copy-start.2
  1.8 24.9 %all_to_all.20 = bf16[32,8,960]{2,1,0:T(8,128)(2,1)S(1)} all-to-all(bf16[32,8,960]{2,1,0:T(8,128)(2,1)S(1)} %shard_map.59), channel_id=1, replica_groups=mesh['vocab'=32,'hidden'=16] {'vocab'}, dimensions={0} | all-to-all | bytes 983040 | tf_op jit(solution)/shard_map/all_to_all | solution.py:30
  26.8 0.0 copy-start.3
  26.8 0.0 copy-done
  26.8 0.0 copy-done.2
  26.8 0.7 copy-done.3
  27.4 0.5 shard_map.60
  28.0 24.8 %all_to_all.21.refs_0_ = bf16[16,16,512]{2,1,0:T(8,128)(2,1)S(1)} all-to-all(bf16[16,16,512]{2,1,0:T(8,128)(2,1)S(1)} %shard_map.60), channel_id=1, replica_groups=mesh['vocab'=32,'hidden'=16] {'hidden'}, dimensions={0} | all-to-all | bytes 524288 | tf_op jit(solution)/shard_map/all_to_all | solution.py:30
  52.8 0.2 shard_map.61
  53.0 23.8 %all_to_all.22.refs_0_ = bf16[8,296,128]{2,1,0:T(8,128)(2,1)S(1)} all-to-all(bf16[8,296,128]{2,1,0:T(8,128)(2,1)S(1)} %shard_map.61), channel_id=1, replica_groups={{0,16,32,48,64,80,96,112},{128,144,160,176,192,208,224,240},{256,272,28..., dimensions={0} | all-to-all | bytes 1212416 | tf_op jit(solution)/shard_map/all_to_all | solution.py:30
  76.9 0.7 shard_map.62
  77.6 9.2 %all_to_all.23.refs_0_ = bf16[4,320,128]{2,1,0:T(8,128)(2,1)S(1)} all-to-all(bf16[4,320,128]{2,1,0:T(8,128)(2,1)S(1)} %shard_map.62), channel_id=1, replica_groups={{0,128,256,384},{16,144,272,400},{32,160,288,416},{48,176,304,432},{64,..., dimensions={0} | all-to-all | bytes 655360 | tf_op jit(solution)/shard_map/all_to_all | solution.py:30
  86.8 0.7 shard_map.63
Async XLA Ops:
  0.6 0.9 %copy-start.1 = (bf16[960,128]{1,0:T(8,128)(2,1)S(1)}, bf16[960,128]{1,0:T(8,128)(2,1)}, u32[]{:S(2)}) copy-start(bf16[960,128]{1,0:T(8,128)(2,1)} %table.1) | copy-start | bytes 737284
  1.8 25.0 %copy-start = (bf16[512,256]{1,0:T(8,128)(2,1)S(1)}, bf16[512,256]{1,0:T(8,128)(2,1)}, u32[]{:S(2)}) copy-start(bf16[512,256]{1,0:T(8,128)(2,1)} %refs_1_.1) | copy-start | bytes 786436
  1.8 25.0 %copy-start.2 = (bf16[128,256]{1,0:T(8,128)(2,1)S(1)}, bf16[128,256]{1,0:T(8,128)(2,1)}, u32[]{:S(2)}) copy-start(bf16[128,256]{1,0:T(8,128)(2,1)} %refs_2_.1) | copy-start | bytes 196612
  26.8 0.7 copy-start.3

commit v4 on v3

v4 whole, which is shorter than its diff:
```python
import jax
import jax.numpy as jnp
from jax import lax
from jax.experimental import pallas as pl
from jax.experimental.pallas import tpu as pltpu
from jax.sharding import PartitionSpec as P

F32, BF16, I32 = jnp.float32, jnp.bfloat16, jnp.int32
LANES, SUBLANES = 128, 8
ALONG_Y = 8


def run(body, out, *args, flops, limit, space=pltpu.VMEM, scratch=()):
    size = lambda a: a.size * a.dtype.itemsize
    vmem = pl.BlockSpec(memory_space=pltpu.VMEM)
    outs = jax.tree.leaves(out)
    if space != pltpu.VMEM:
        args = [pltpu.with_memory_space_constraint(a, space) for a in args]
    return pl.pallas_call(
        body,
        out_shape=out,
        in_specs=[pl.BlockSpec(memory_space=space)] * len(args),
        out_specs=jax.tree.map(lambda _: vmem, out),
        scratch_shapes=scratch,
        compiler_params=pltpu.CompilerParams(vmem_limit_bytes=limit * 2**20),
        cost_estimate=pl.CostEstimate(
            flops=flops, bytes_accessed=sum(map(size, [*args, *outs])), transcendentals=0
        ),
    )(*args)


def exchange(blocks, axis, groups=None):
    return lax.all_to_all(blocks, axis, split_axis=0, concat_axis=0, tiled=True, axis_index_groups=groups)


def contract_last(a, b):
    return lax.dot_general(a, b, (((1,), (1,)), ((), ())), preferred_element_type=F32)


def one_hot_rows(which, rows):
    shape = (rows, which.shape[1])
    return (lax.broadcasted_iota(I32, shape, 0) == which).astype(F32).astype(BF16)


def owner_and_row(token, rows):
    owner = ((token >> 6) * 4370) >> 16
    return owner, token - owner * rows


def columns_body(table_there, ids_there, out, places, digits, table, ids, arrivals):
    copies = [
        pltpu.make_async_copy(table_there, table, arrivals.at[0]),
        pltpu.make_async_copy(ids_there, ids, arrivals.at[1]),
    ]
    for copy in copies:
        copy.start()
    copies[1].wait()
    owner, row = owner_and_row(ids[...], table.shape[0])
    digits[...] = jnp.concatenate([owner * 8 + (row >> 7), row & 127], axis=0).astype(F32)
    for c in range(ids.shape[0]):
        at = slice(c * LANES, (c + 1) * LANES)
        places[0:1, at] = owner[c : c + 1]
        places[1:2, at] = row[c : c + 1]
    copies[0].wait()
    width = out.shape[1]
    first = lax.axis_index("hidden") * width
    shape = (width, table.shape[1])
    lane = lax.broadcasted_iota(I32, shape, 1)
    pick = (lane == lax.broadcasted_iota(I32, shape, 0) + first).astype(F32).astype(BF16)
    mine = contract_last(pick, table[...]).astype(BF16)
    for peer in range(out.shape[0]):
        out[peer] = mine


def lookup_body(owners, table, places, projection, grad_out, out):
    width = out.shape[1] // 2
    count = places.shape[1]
    partial = contract_last(projection[...], grad_out[...])
    owner, row = places[0:1, :], places[1:2, :]
    every = jnp.dot(table[...], one_hot_rows(row, table.shape[1]), preferred_element_type=F32)
    total = jnp.zeros((width, count), F32)
    for v in range(owners):
        total = jnp.where(owner == v, every[v * width : (v + 1) * width], total)
    mine = total.astype(BF16)
    for peer in range(out.shape[0]):
        out[peer, :width] = mine
        out[peer, width:] = partial[peer * width : (peer + 1) * width].astype(BF16)


def rows_of_lanes(value):
    return [value[:, j : j + LANES] for j in range(0, value.shape[1], LANES)]


def products_body(arrived, grad_out, digits, out):
    peers = arrived.shape[0]
    width = arrived.shape[1] // 2
    embedded = jnp.concatenate([arrived[p, :width] for p in range(peers)], axis=0)
    product = jnp.dot(embedded, grad_out[...], preferred_element_type=F32)
    product = jnp.concatenate(rows_of_lanes(product), axis=0).astype(BF16)
    grad = arrived[0, width:].astype(F32)
    for peer in range(1, peers):
        grad = grad + arrived[peer, width:].astype(F32)
    small = [part.astype(BF16) for part in [*rows_of_lanes(grad), digits[...]]]
    members = out.shape[0]
    piece = product.shape[0] // members
    for peer in range(members):
        out[peer, :piece] = product[peer * piece : (peer + 1) * piece]
        for c, part in enumerate(small):
            at = piece + c * SUBLANES
            out[peer, at : at + SUBLANES] = part


def group_sums_body(piece, arrived, out):
    members, owners = arrived.shape[0], out.shape[0]
    chunks = (arrived.shape[1] - piece) // SUBLANES - 1
    vocab = lax.axis_index("vocab")
    member = (vocab // ALONG_Y) * 2 + (vocab & 1)

    total = arrived[0, :piece].astype(F32)
    for peer in range(1, members):
        total = total + arrived[peer, :piece].astype(F32)
    total = total.astype(BF16)

    sums = jnp.zeros((owners * SUBLANES, LANES), F32)
    for peer in range(members):
        at = piece + chunks * SUBLANES
        digits = arrived[peer, at : at + SUBLANES].astype(F32).astype(I32)
        high, low = digits[:chunks], digits[chunks:]
        owner = jnp.where((high & 7) == member, high >> 3, -1)
        left, right = [], []
        for c in range(chunks):
            start = piece + c * SUBLANES
            part = arrived[peer, start : start + SUBLANES].astype(F32)
            owner_c = jnp.broadcast_to(owner[c : c + 1], part.shape)
            left.append(
                jnp.concatenate([jnp.where(owner_c == v, part, 0.0) for v in range(owners)], axis=0).astype(BF16)
            )
            right.append(one_hot_rows(low[c : c + 1], LANES))
        sums = sums + contract_last(jnp.concatenate(left, axis=1), jnp.concatenate(right, axis=1))
    sums = sums.astype(BF16)
    for v in range(owners):
        out[v, :piece] = total
        out[v, piece:] = sums[v * SUBLANES : (v + 1) * SUBLANES]


def last_sums_body(piece, arrived, table_grad, projection_grad):
    owners = arrived.shape[0]
    depth = projection_grad.shape[0]
    rows = table_grad.shape[1]
    members = depth * projection_grad.shape[1] // LANES // piece
    for member in range(members):
        first = (member >> 1) * ALONG_Y + (member & 1)
        total = arrived[first].astype(F32)
        for peer in range(first + 2, first + ALONG_Y, 2):
            total = total + arrived[peer].astype(F32)
        at, lane = member * piece % depth, member * piece // depth * LANES
        projection_grad[at : at + piece, lane : lane + LANES] = total[:piece]
        wide = min(LANES, rows - member * LANES)
        table_grad[:, member * LANES : member * LANES + wide] = total[piece:, :wide]


def on_device(token_ids, table, projection, grad_out):
    owners, peers = lax.axis_size("vocab"), lax.axis_size("hidden")
    along_x = owners // ALONG_Y
    members = 2 * along_x
    groups = [
        [x * ALONG_Y + y + bit for x in range(along_x) for bit in range(2)] for y in range(0, ALONG_Y, 2)
    ]
    rows, depth = table.shape
    width = depth // peers
    count = token_ids.shape[0]
    hidden = projection.shape[1]
    piece = depth * hidden // LANES // members
    chunks = count // LANES
    S = jax.ShapeDtypeStruct

    by_lane = token_ids.reshape(chunks, LANES)
    columns, places, digits = run(
        columns_body,
        (S((owners, width, rows), BF16), S((2, count), I32), S((2 * chunks, LANES), F32)),
        table,
        by_lane,
        flops=2 * depth * rows * width,
        limit=4,
        space=pltpu.HBM,
        scratch=[
            pltpu.VMEM(table.shape, table.dtype),
            pltpu.VMEM(by_lane.shape, I32),
            pltpu.SemaphoreType.DMA((2,)),
        ],
    )
    columns = exchange(columns, "vocab").reshape(owners * width, rows)

    def lookup(*refs):
        lookup_body(owners, *refs)

    def group_sums(*refs):
        group_sums_body(piece, *refs)

    def last_sums(*refs):
        last_sums_body(piece, *refs)

    looked = run(
        lookup,
        S((peers, 2 * width, count), BF16),
        columns,
        places,
        projection,
        grad_out,
        flops=2 * owners * width * rows * count + 2 * depth * count * hidden,
        limit=8,
    )
    looked = exchange(looked, "hidden")

    made = run(
        products_body,
        S((members, piece + (chunks + 1) * SUBLANES, LANES), BF16),
        looked,
        grad_out,
        digits,
        flops=2 * depth * count * hidden,
        limit=8,
    )
    made = exchange(made, "vocab", groups)

    summed = run(
        group_sums,
        S((owners, piece + SUBLANES, LANES), BF16),
        made,
        flops=2 * members * count * owners * SUBLANES * LANES,
        limit=8,
    )
    summed = exchange(summed, "vocab")

    table_grad, projection_grad = run(
        last_sums, (S((width, rows), F32), S((depth, hidden), F32)), summed, flops=summed.size, limit=8
    )
    return table_grad.T, projection_grad


def solution(mesh):
    placed = (P("vocab"), P("vocab", None), P(None, "hidden"), P("vocab", "hidden"))
    return jax.shard_map(
        on_device,
        mesh=mesh,
        in_specs=placed,
        out_specs=(P("vocab", "hidden"), P(None, "hidden")),
        check_vma=False,
    )
```

time: 87.8 us -> 81.1 us (0.924)
  the two profiles are of different devices: /device:TPU:1 before, /device:TPU:8 now
where the time goes in v4:
time: 81.1 us; the launch traced here: 80.8 us
  blocking collectives  76.8 us (95%)
  Pallas kernels  3.31 us (4%)
    all_to_all x4, blocking collectives, exchange(): lax.all_to_all(blocks, axis, split_axis=0, concat_axis=0, tiled=True, axi...  76.8 us
    pallas_call x5, Pallas kernels, run(): pl.pallas_call(body, out_shape=out, in_specs=[pl.BlockSpec(memory_space=s...  3.31 us

profile of v4, /device:TPU:8, one launch (start us, length us, event | category | flops | bytes accessed | tf_op | source)
XLA Modules:
  0.0 80.8 jit_solution(9886209976092770109)
XLA Ops:
  0.6 1.2 %shard_map.59 = (bf16[32,8,960]{2,1,0:T(8,128)(2,1)S(1)}, s32[2,512]{1,0:T(2,128)S(1)}, f32[8,128]{1,0:T(8,128)S(1)}) custom-call(bf16[960,128]{1,0:T(8,128)(2,1)} %table_there.1, s32[4,128]{1,0:T(4,128)} %bitcast.4), custom_call_target="tpu_custom_call" | custom-call | flops 1966080 | bytes 747520 | tf_op jit(solution)/shard_map/pallas_call | solution.py:19
  1.8 0.0 copy-start
  1.8 0.0 copy-start.1
  1.8 27.7 %all_to_all.20 = bf16[32,8,960]{2,1,0:T(8,128)(2,1)S(1)} all-to-all(bf16[32,8,960]{2,1,0:T(8,128)(2,1)S(1)} %get-tuple-element.7), channel_id=1, replica_groups=mesh['vocab'=32,'hidden'=16] {'vocab'}, dimensions={0} | all-to-all | bytes 983040 | tf_op jit(solution)/shard_map/all_to_all | solution.py:33
  29.6 0.0 copy-done
  29.6 0.0 copy-done.1
  29.6 0.5 shard_map.60
  30.1 21.4 %all_to_all.21.arrived = bf16[16,16,512]{2,1,0:T(8,128)(2,1)S(1)} all-to-all(bf16[16,16,512]{2,1,0:T(8,128)(2,1)S(1)} %shard_map.60), channel_id=1, replica_groups=mesh['vocab'=32,'hidden'=16] {'hidden'}, dimensions={0} | all-to-all | bytes 524288 | tf_op jit(solution)/shard_map/all_to_all | solution.py:33
  51.5 0.2 shard_map.61
  51.7 9.8 %all_to_all.22.refs_0_ = bf16[8,72,128]{2,1,0:T(8,128)(2,1)S(1)} all-to-all(bf16[8,72,128]{2,1,0:T(8,128)(2,1)S(1)} %shard_map.61), channel_id=1, replica_groups={{0,16,128,144,256,272,384,400},{32,48,160,176,288,304,416,432},{64,80,1..., dimensions={0} | all-to-all | bytes 294912 | tf_op jit(solution)/shard_map/all_to_all | solution.py:33
  61.5 0.7 shard_map.62
  62.2 17.9 %all_to_all.23.refs_0_ = bf16[32,40,128]{2,1,0:T(8,128)(2,1)S(1)} all-to-all(bf16[32,40,128]{2,1,0:T(8,128)(2,1)S(1)} %shard_map.62), channel_id=1, replica_groups=mesh['vocab'=32,'hidden'=16] {'vocab'}, dimensions={0} | all-to-all | bytes 655360 | tf_op jit(solution)/shard_map/all_to_all | solution.py:33
  80.1 0.7 shard_map.63
Async XLA Ops:
  1.8 27.7 %copy-start = (bf16[512,256]{1,0:T(8,128)(2,1)S(1)}, bf16[512,256]{1,0:T(8,128)(2,1)}, u32[]{:S(2)}) copy-start(bf16[512,256]{1,0:T(8,128)(2,1)} %grad_out.1) | copy-start | bytes 786436
  1.8 27.7 %copy-start.1 = (bf16[128,256]{1,0:T(8,128)(2,1)S(1)}, bf16[128,256]{1,0:T(8,128)(2,1)}, u32[]{:S(2)}) copy-start(bf16[128,256]{1,0:T(8,128)(2,1)} %refs_2_.1) | copy-start | bytes 196612

commit v5 on v4

--- a/solution.py
+++ b/solution.py
@@ -7,6 +7,7 @@
 
 F32, BF16, I32 = jnp.float32, jnp.bfloat16, jnp.int32
 LANES, SUBLANES = 128, 8
+CUT = 256
 ALONG_Y = 8
 
 
@@ -37,9 +38,17 @@
     return lax.dot_general(a, b, (((1,), (1,)), ((), ())), preferred_element_type=F32)
 
 
-def one_hot_rows(which, rows):
-    shape = (rows, which.shape[1])
-    return (lax.broadcasted_iota(I32, shape, 0) == which).astype(F32).astype(BF16)
+def small(value):
+    return value.astype(F32).astype(BF16)
+
+
+def row_numbers(rows, count):
+    return small(lax.broadcasted_iota(I32, (rows, count), 0))
+
+
+def one_hot_rows(which, numbers):
+    which = jnp.broadcast_to(small(which), numbers.shape)
+    return jnp.where(which == numbers, jnp.ones_like(numbers), jnp.zeros_like(numbers))
 
 
 def owner_and_row(token, rows):
@@ -48,28 +57,32 @@
 
 
 def columns_body(table_there, ids_there, out, places, digits, table, ids, arrivals):
+    rows = table.shape[0]
+    cuts = [(at, min(CUT, rows - at)) for at in range(0, rows, CUT)]
     copies = [
-        pltpu.make_async_copy(table_there, table, arrivals.at[0]),
-        pltpu.make_async_copy(ids_there, ids, arrivals.at[1]),
+        pltpu.make_async_copy(table_there.at[pl.ds(at, size)], table.at[pl.ds(at, size)], arrivals.at[i])
+        for i, (at, size) in enumerate(cuts)
     ]
-    for copy in copies:
+    ids_copy = pltpu.make_async_copy(ids_there, ids, arrivals.at[len(cuts)])
+    for copy in [*copies, ids_copy]:
         copy.start()
-    copies[1].wait()
+    ids_copy.wait()
     owner, row = owner_and_row(ids[...], table.shape[0])
     digits[...] = jnp.concatenate([owner * 8 + (row >> 7), row & 127], axis=0).astype(F32)
     for c in range(ids.shape[0]):
         at = slice(c * LANES, (c + 1) * LANES)
         places[0:1, at] = owner[c : c + 1]
         places[1:2, at] = row[c : c + 1]
-    copies[0].wait()
     width = out.shape[1]
     first = lax.axis_index("hidden") * width
     shape = (width, table.shape[1])
     lane = lax.broadcasted_iota(I32, shape, 1)
     pick = (lane == lax.broadcasted_iota(I32, shape, 0) + first).astype(F32).astype(BF16)
-    mine = contract_last(pick, table[...]).astype(BF16)
-    for peer in range(out.shape[0]):
-        out[peer] = mine
+    for copy, (at, size) in zip(copies, cuts):
+        copy.wait()
+        mine = contract_last(pick, table[at : at + size]).astype(BF16)
+        for peer in range(out.shape[0]):
+            out[peer, :, at : at + size] = mine
 
 
 def lookup_body(owners, table, places, projection, grad_out, out):
@@ -77,7 +90,10 @@
     count = places.shape[1]
     partial = contract_last(projection[...], grad_out[...])
     owner, row = places[0:1, :], places[1:2, :]
-    every = jnp.dot(table[...], one_hot_rows(row, table.shape[1]), preferred_element_type=F32)
+    numbers = row_numbers(LANES, count)
+    rows = table.shape[1]
+    hot = [one_hot_rows(row - at, numbers[: min(LANES, rows - at)]) for at in range(0, rows, LANES)]
+    every = jnp.dot(table[...], jnp.concatenate(hot, axis=0), preferred_element_type=F32)
     total = jnp.zeros((width, count), F32)
     for v in range(owners):
         total = jnp.where(owner == v, every[v * width : (v + 1) * width], total)
@@ -100,12 +116,12 @@
     grad = arrived[0, width:].astype(F32)
     for peer in range(1, peers):
         grad = grad + arrived[peer, width:].astype(F32)
-    small = [part.astype(BF16) for part in [*rows_of_lanes(grad), digits[...]]]
+    lines = [part.astype(BF16) for part in [*rows_of_lanes(grad), digits[...]]]
     members = out.shape[0]
     piece = product.shape[0] // members
     for peer in range(members):
         out[peer, :piece] = product[peer * piece : (peer + 1) * piece]
-        for c, part in enumerate(small):
+        for c, part in enumerate(lines):
             at = piece + c * SUBLANES
             out[peer, at : at + SUBLANES] = part
 
@@ -121,21 +137,23 @@
         total = total + arrived[peer, :piece].astype(F32)
     total = total.astype(BF16)
 
+    numbers = row_numbers(LANES, LANES)
+    second = small(lax.broadcasted_iota(I32, (2 * SUBLANES, LANES), 0) >> 3)
     sums = jnp.zeros((owners * SUBLANES, LANES), F32)
     for peer in range(members):
         at = piece + chunks * SUBLANES
         digits = arrived[peer, at : at + SUBLANES].astype(F32).astype(I32)
         high, low = digits[:chunks], digits[chunks:]
-        owner = jnp.where((high & 7) == member, high >> 3, -1)
+        owner = jnp.where((high & 7) == member, high >> 3, -2)
         left, right = [], []
         for c in range(chunks):
             start = piece + c * SUBLANES
-            part = arrived[peer, start : start + SUBLANES].astype(F32)
-            owner_c = jnp.broadcast_to(owner[c : c + 1], part.shape)
-            left.append(
-                jnp.concatenate([jnp.where(owner_c == v, part, 0.0) for v in range(owners)], axis=0).astype(BF16)
-            )
-            right.append(one_hot_rows(low[c : c + 1], LANES))
+            part = arrived[peer, start : start + SUBLANES]
+            twice = jnp.concatenate([part, part], axis=0)
+            nought = jnp.zeros_like(twice)
+            pair = jnp.broadcast_to(small(owner[c : c + 1]), twice.shape) - second
+            left.append(jnp.concatenate([jnp.where(pair == v, twice, nought) for v in range(0, owners, 2)], axis=0))
+            right.append(one_hot_rows(low[c : c + 1], numbers))
         sums = sums + contract_last(jnp.concatenate(left, axis=1), jnp.concatenate(right, axis=1))
     sums = sums.astype(BF16)
     for v in range(owners):
@@ -186,7 +204,7 @@
         scratch=[
             pltpu.VMEM(table.shape, table.dtype),
             pltpu.VMEM(by_lane.shape, I32),
-            pltpu.SemaphoreType.DMA((2,)),
+            pltpu.SemaphoreType.DMA((-(-rows // CUT) + 1,)),
         ],
     )
     columns = exchange(columns, "vocab").reshape(owners * width, rows)

time: 81.1 us -> 81.5 us (level)
  no operation moved by 1% of the time
where the time goes in v5:
time: 81.5 us; the launch traced here: 81.2 us
  blocking collectives  76.8 us (94%)
  Pallas kernels  3.67 us (5%)
    all_to_all x4, blocking collectives, exchange(): lax.all_to_all(blocks, axis, split_axis=0, concat_axis=0, tiled=True, axi...  76.8 us
    pallas_call x5, Pallas kernels, run(): pl.pallas_call(body, out_shape=out, in_specs=[pl.BlockSpec(memory_space=s...  3.67 us

profile of v5, /device:TPU:8, one launch (start us, length us, event | category | flops | bytes accessed | tf_op | source)
XLA Modules:
  0.0 81.2 jit_solution(7982061975310383002)
XLA Ops:
  0.6 1.6 %shard_map.59 = (bf16[32,8,960]{2,1,0:T(8,128)(2,1)S(1)}, s32[2,512]{1,0:T(2,128)S(1)}, f32[8,128]{1,0:T(8,128)S(1)}) custom-call(bf16[960,128]{1,0:T(8,128)(2,1)} %table_there.1, s32[4,128]{1,0:T(4,128)} %bitcast.4), custom_call_target="tpu_custom_call" | custom-call | flops 1966080 | bytes 747520 | tf_op jit(solution)/shard_map/pallas_call | solution.py:20
  2.2 0.0 copy-start
  2.2 0.0 copy-start.1
  2.2 27.7 %all_to_all.20 = bf16[32,8,960]{2,1,0:T(8,128)(2,1)S(1)} all-to-all(bf16[32,8,960]{2,1,0:T(8,128)(2,1)S(1)} %get-tuple-element.7), channel_id=1, replica_groups=mesh['vocab'=32,'hidden'=16] {'vocab'}, dimensions={0} | all-to-all | bytes 983040 | tf_op jit(solution)/shard_map/all_to_all | solution.py:34
  29.9 0.0 copy-done
  29.9 0.0 copy-done.1
  29.9 0.5 shard_map.60
  30.5 21.4 %all_to_all.21.arrived = bf16[16,16,512]{2,1,0:T(8,128)(2,1)S(1)} all-to-all(bf16[16,16,512]{2,1,0:T(8,128)(2,1)S(1)} %shard_map.60), channel_id=1, replica_groups=mesh['vocab'=32,'hidden'=16] {'hidden'}, dimensions={0} | all-to-all | bytes 524288 | tf_op jit(solution)/shard_map/all_to_all | solution.py:34
  51.8 0.2 shard_map.61
  52.0 9.8 %all_to_all.22.refs_0_ = bf16[8,72,128]{2,1,0:T(8,128)(2,1)S(1)} all-to-all(bf16[8,72,128]{2,1,0:T(8,128)(2,1)S(1)} %shard_map.61), channel_id=1, replica_groups={{0,16,128,144,256,272,384,400},{32,48,160,176,288,304,416,432},{64,80,1..., dimensions={0} | all-to-all | bytes 294912 | tf_op jit(solution)/shard_map/all_to_all | solution.py:34
  61.8 0.7 shard_map.62
  62.6 17.9 %all_to_all.23.refs_0_ = bf16[32,40,128]{2,1,0:T(8,128)(2,1)S(1)} all-to-all(bf16[32,40,128]{2,1,0:T(8,128)(2,1)S(1)} %shard_map.62), channel_id=1, replica_groups=mesh['vocab'=32,'hidden'=16] {'vocab'}, dimensions={0} | all-to-all | bytes 655360 | tf_op jit(solution)/shard_map/all_to_all | solution.py:34
  80.5 0.7 shard_map.63
Async XLA Ops:
  2.2 27.7 %copy-start = (bf16[512,256]{1,0:T(8,128)(2,1)S(1)}, bf16[512,256]{1,0:T(8,128)(2,1)}, u32[]{:S(2)}) copy-start(bf16[512,256]{1,0:T(8,128)(2,1)} %grad_out.1) | copy-start | bytes 786436
  2.2 27.7 %copy-start.1 = (bf16[128,256]{1,0:T(8,128)(2,1)S(1)}, bf16[128,256]{1,0:T(8,128)(2,1)}, u32[]{:S(2)}) copy-start(bf16[128,256]{1,0:T(8,128)(2,1)} %refs_2_.1) | copy-start | bytes 196612

commit v6 on v4

--- a/solution.py
+++ b/solution.py
@@ -37,9 +37,17 @@
     return lax.dot_general(a, b, (((1,), (1,)), ((), ())), preferred_element_type=F32)
 
 
-def one_hot_rows(which, rows):
-    shape = (rows, which.shape[1])
-    return (lax.broadcasted_iota(I32, shape, 0) == which).astype(F32).astype(BF16)
+def small(value):
+    return value.astype(F32).astype(BF16)
+
+
+def row_numbers(rows, count):
+    return small(lax.broadcasted_iota(I32, (rows, count), 0))
+
+
+def one_hot_rows(which, numbers):
+    which = jnp.broadcast_to(small(which), numbers.shape)
+    return jnp.where(which == numbers, jnp.ones_like(numbers), jnp.zeros_like(numbers))
 
 
 def owner_and_row(token, rows):
@@ -77,7 +85,10 @@
     count = places.shape[1]
     partial = contract_last(projection[...], grad_out[...])
     owner, row = places[0:1, :], places[1:2, :]
-    every = jnp.dot(table[...], one_hot_rows(row, table.shape[1]), preferred_element_type=F32)
+    numbers = row_numbers(LANES, count)
+    rows = table.shape[1]
+    hot = [one_hot_rows(row - at, numbers[: min(LANES, rows - at)]) for at in range(0, rows, LANES)]
+    every = jnp.dot(table[...], jnp.concatenate(hot, axis=0), preferred_element_type=F32)
     total = jnp.zeros((width, count), F32)
     for v in range(owners):
         total = jnp.where(owner == v, every[v * width : (v + 1) * width], total)
@@ -100,12 +111,12 @@
     grad = arrived[0, width:].astype(F32)
     for peer in range(1, peers):
         grad = grad + arrived[peer, width:].astype(F32)
-    small = [part.astype(BF16) for part in [*rows_of_lanes(grad), digits[...]]]
+    lines = [part.astype(BF16) for part in [*rows_of_lanes(grad), digits[...]]]
     members = out.shape[0]
     piece = product.shape[0] // members
     for peer in range(members):
         out[peer, :piece] = product[peer * piece : (peer + 1) * piece]
-        for c, part in enumerate(small):
+        for c, part in enumerate(lines):
             at = piece + c * SUBLANES
             out[peer, at : at + SUBLANES] = part
 
@@ -121,26 +132,32 @@
         total = total + arrived[peer, :piece].astype(F32)
     total = total.astype(BF16)
 
-    sums = jnp.zeros((owners * SUBLANES, LANES), F32)
+    numbers = row_numbers(2 * LANES, LANES)
+    second = small(lax.broadcasted_iota(I32, (2 * SUBLANES, LANES), 0) >> 3)
+    sums = jnp.zeros((owners // 2 * SUBLANES, 2 * LANES), F32)
     for peer in range(members):
         at = piece + chunks * SUBLANES
         digits = arrived[peer, at : at + SUBLANES].astype(F32).astype(I32)
         high, low = digits[:chunks], digits[chunks:]
-        owner = jnp.where((high & 7) == member, high >> 3, -1)
+        two_owners = jnp.where((high & 7) == member, high >> 4, -2)
+        row = ((high >> 3) & 1) * LANES + low
         left, right = [], []
         for c in range(chunks):
             start = piece + c * SUBLANES
-            part = arrived[peer, start : start + SUBLANES].astype(F32)
-            owner_c = jnp.broadcast_to(owner[c : c + 1], part.shape)
+            part = arrived[peer, start : start + SUBLANES]
+            twice = jnp.concatenate([part, part], axis=0)
+            nought = jnp.zeros_like(twice)
+            pair = jnp.broadcast_to(small(two_owners[c : c + 1]), twice.shape) - second
             left.append(
-                jnp.concatenate([jnp.where(owner_c == v, part, 0.0) for v in range(owners)], axis=0).astype(BF16)
+                jnp.concatenate([jnp.where(pair == v, twice, nought) for v in range(0, owners // 2, 2)], axis=0)
             )
-            right.append(one_hot_rows(low[c : c + 1], LANES))
+            right.append(one_hot_rows(row[c : c + 1], numbers))
         sums = sums + contract_last(jnp.concatenate(left, axis=1), jnp.concatenate(right, axis=1))
     sums = sums.astype(BF16)
     for v in range(owners):
         out[v, :piece] = total
-        out[v, piece:] = sums[v * SUBLANES : (v + 1) * SUBLANES]
+        at, lane = v // 2 * SUBLANES, v % 2 * LANES
+        out[v, piece:] = sums[at : at + SUBLANES, lane : lane + LANES]
 
 
 def last_sums_body(piece, arrived, table_grad, projection_grad):

time: 81.1 us -> 81.2 us (level)
  no operation moved by 1% of the time
where the time goes in v6:
time: 81.2 us; the launch traced here: 80.9 us
  blocking collectives  76.8 us (95%)
  Pallas kernels  3.41 us (4%)
    all_to_all x4, blocking collectives, exchange(): lax.all_to_all(blocks, axis, split_axis=0, concat_axis=0, tiled=True, axi...  76.8 us
    pallas_call x5, Pallas kernels, run(): pl.pallas_call(body, out_shape=out, in_specs=[pl.BlockSpec(memory_space=s...  3.41 us

profile of v6, /device:TPU:8, one launch (start us, length us, event | category | flops | bytes accessed | tf_op | source)
XLA Modules:
  0.0 80.9 jit_solution(18011988047105008418)
XLA Ops:
  0.6 1.2 %shard_map.59 = (bf16[32,8,960]{2,1,0:T(8,128)(2,1)S(1)}, s32[2,512]{1,0:T(2,128)S(1)}, f32[8,128]{1,0:T(8,128)S(1)}) custom-call(bf16[960,128]{1,0:T(8,128)(2,1)} %table_there.1, s32[4,128]{1,0:T(4,128)} %bitcast.4), custom_call_target="tpu_custom_call" | custom-call | flops 1966080 | bytes 747520 | tf_op jit(solution)/shard_map/pallas_call | solution.py:19
  1.8 0.0 copy-start
  1.8 0.0 copy-start.1
  1.8 27.7 %all_to_all.20 = bf16[32,8,960]{2,1,0:T(8,128)(2,1)S(1)} all-to-all(bf16[32,8,960]{2,1,0:T(8,128)(2,1)S(1)} %get-tuple-element.7), channel_id=1, replica_groups=mesh['vocab'=32,'hidden'=16] {'vocab'}, dimensions={0} | all-to-all | bytes 983040 | tf_op jit(solution)/shard_map/all_to_all | solution.py:33
  29.6 0.0 copy-done
  29.6 0.0 copy-done.1
  29.6 0.5 shard_map.60
  30.1 21.4 %all_to_all.21.arrived = bf16[16,16,512]{2,1,0:T(8,128)(2,1)S(1)} all-to-all(bf16[16,16,512]{2,1,0:T(8,128)(2,1)S(1)} %shard_map.60), channel_id=1, replica_groups=mesh['vocab'=32,'hidden'=16] {'hidden'}, dimensions={0} | all-to-all | bytes 524288 | tf_op jit(solution)/shard_map/all_to_all | solution.py:33
  51.5 0.2 shard_map.61
  51.6 9.8 %all_to_all.22.refs_0_ = bf16[8,72,128]{2,1,0:T(8,128)(2,1)S(1)} all-to-all(bf16[8,72,128]{2,1,0:T(8,128)(2,1)S(1)} %shard_map.61), channel_id=1, replica_groups={{0,16,128,144,256,272,384,400},{32,48,160,176,288,304,416,432},{64,80,1..., dimensions={0} | all-to-all | bytes 294912 | tf_op jit(solution)/shard_map/all_to_all | solution.py:33
  61.5 0.8 %shard_map.62 = bf16[32,40,128]{2,1,0:T(8,128)(2,1)S(1)} custom-call(bf16[8,72,128]{2,1,0:T(8,128)(2,1)S(1)} %all_to_all.22.refs_0_), custom_call_target="tpu_custom_call" | custom-call | flops 268435456 | bytes 475136 | tf_op jit(solution)/shard_map/pallas_call | solution.py:19
  62.3 17.9 %all_to_all.23.refs_0_ = bf16[32,40,128]{2,1,0:T(8,128)(2,1)S(1)} all-to-all(bf16[32,40,128]{2,1,0:T(8,128)(2,1)S(1)} %shard_map.62), channel_id=1, replica_groups=mesh['vocab'=32,'hidden'=16] {'vocab'}, dimensions={0} | all-to-all | bytes 655360 | tf_op jit(solution)/shard_map/all_to_all | solution.py:33
  80.2 0.7 shard_map.63
Async XLA Ops:
  1.8 27.7 %copy-start = (bf16[512,256]{1,0:T(8,128)(2,1)S(1)}, bf16[512,256]{1,0:T(8,128)(2,1)}, u32[]{:S(2)}) copy-start(bf16[512,256]{1,0:T(8,128)(2,1)} %grad_out.1) | copy-start | bytes 786436
  1.8 27.7 %copy-start.1 = (bf16[128,256]{1,0:T(8,128)(2,1)S(1)}, bf16[128,256]{1,0:T(8,128)(2,1)}, u32[]{:S(2)}) copy-start(bf16[128,256]{1,0:T(8,128)(2,1)} %refs_2_.1) | copy-start | bytes 196612

commit v7 on v4

--- a/solution.py
+++ b/solution.py
@@ -62,12 +62,16 @@
         places[0:1, at] = owner[c : c + 1]
         places[1:2, at] = row[c : c + 1]
     copies[0].wait()
-    width = out.shape[1]
+    width = out.shape[1] * 2
     first = lax.axis_index("hidden") * width
     shape = (width, table.shape[1])
     lane = lax.broadcasted_iota(I32, shape, 1)
     pick = (lane == lax.broadcasted_iota(I32, shape, 0) + first).astype(F32).astype(BF16)
-    mine = contract_last(pick, table[...]).astype(BF16)
+    mine = contract_last(pick, table[...])
+    half, whole = width // 2, table.shape[0] // LANES * LANES
+    mine = jnp.concatenate(
+        [mine[:half, :whole], mine[half:, :whole], mine[:half, whole:], mine[half:, whole:]], axis=1
+    ).astype(BF16)
     for peer in range(out.shape[0]):
         out[peer] = mine
 
@@ -77,10 +81,28 @@
     count = places.shape[1]
     partial = contract_last(projection[...], grad_out[...])
     owner, row = places[0:1, :], places[1:2, :]
-    every = jnp.dot(table[...], one_hot_rows(row, table.shape[1]), preferred_element_type=F32)
-    total = jnp.zeros((width, count), F32)
-    for v in range(owners):
-        total = jnp.where(owner == v, every[v * width : (v + 1) * width], total)
+    half = width // 2
+    lines = table.shape[2]
+    rows = lines // 2
+    whole = rows // LANES * LANES
+    held = table[...].reshape(owners * half, lines)
+    both = jnp.concatenate([held[:, :whole], held[:, whole : 2 * whole]], axis=0)
+    every = jnp.dot(both, one_hot_rows(row, whole), preferred_element_type=F32)
+    rest = held[:, 2 * whole :]
+    left = row - whole
+    right = jnp.where(left >= 0, left + (rows - whole), -1)
+    tails = [one_hot_rows(left, LANES // 2), one_hot_rows(right, LANES)]
+    tails[0] = jnp.concatenate([tails[0], jnp.zeros_like(tails[0])], axis=0)
+    first = every[: owners * half] + jnp.dot(rest, tails[0], preferred_element_type=F32)
+    other = every[owners * half :] + jnp.dot(rest, tails[1], preferred_element_type=F32)
+    pair = owner - (lax.broadcasted_iota(I32, (width, count), 0) >= half).astype(I32)
+    sums = []
+    for found in (first, other):
+        total = jnp.zeros((width, count), F32)
+        for v in range(0, owners, 2):
+            total = jnp.where(pair == v, found[v * half : (v + 2) * half], total)
+        sums.append(total[:half] + total[half:])
+    total = jnp.concatenate(sums, axis=0)
     mine = total.astype(BF16)
     for peer in range(out.shape[0]):
         out[peer, :width] = mine
@@ -177,7 +199,7 @@
     by_lane = token_ids.reshape(chunks, LANES)
     columns, places, digits = run(
         columns_body,
-        (S((owners, width, rows), BF16), S((2, count), I32), S((2 * chunks, LANES), F32)),
+        (S((owners, width // 2, 2 * rows), BF16), S((2, count), I32), S((2 * chunks, LANES), F32)),
         table,
         by_lane,
         flops=2 * depth * rows * width,
@@ -189,7 +211,7 @@
             pltpu.SemaphoreType.DMA((2,)),
         ],
     )
-    columns = exchange(columns, "vocab").reshape(owners * width, rows)
+    columns = exchange(columns, "vocab")
 
     def lookup(*refs):
         lookup_body(owners, *refs)

time: 81.1 us -> 80.5 us (level)
  no operation moved by 1% of the time
where the time goes in v7:
time: 80.5 us; the launch traced here: 80.3 us
  blocking collectives  76.1 us (95%)
  Pallas kernels  3.49 us (4%)
    all_to_all x4, blocking collectives, exchange(): lax.all_to_all(blocks, axis, split_axis=0, concat_axis=0, tiled=True, axi...  76.1 us
    pallas_call x5, Pallas kernels, run(): pl.pallas_call(body, out_shape=out, in_specs=[pl.BlockSpec(memory_space=s...  3.49 us

profile of v7, /device:TPU:8, one launch (start us, length us, event | category | flops | bytes accessed | tf_op | source)
XLA Modules:
  0.0 80.3 jit_solution(7114986180647215692)
XLA Ops:
  0.6 1.2 %shard_map.59 = (bf16[32,4,1920]{2,1,0:T(4,128)(2,1)S(1)}, s32[2,512]{1,0:T(2,128)S(1)}, f32[8,128]{1,0:T(8,128)S(1)}) custom-call(bf16[960,128]{1,0:T(8,128)(2,1)} %table_there.1, s32[4,128]{1,0:T(4,128)} %bitcast.2), custom_call_target="tpu_custom_call" | custom-call | flops 1966080 | bytes 747520 | tf_op jit(solution)/shard_map/pallas_call | solution.py:19
  1.9 0.0 copy-start
  1.9 0.0 copy-start.1
  1.9 27.1 %all_to_all.20.refs_0_ = bf16[32,4,1920]{2,1,0:T(4,128)(2,1)S(1)} all-to-all(bf16[32,4,1920]{2,1,0:T(4,128)(2,1)S(1)} %get-tuple-element.7), channel_id=1, replica_groups=mesh['vocab'=32,'hidden'=16] {'vocab'}, dimensions={0} | all-to-all | bytes 983040 | tf_op jit(solution)/shard_map/all_to_all | solution.py:33
  29.0 0.0 copy-done
  29.0 0.0 copy-done.1
  29.0 0.7 shard_map.60
  29.6 21.4 %all_to_all.21.arrived = bf16[16,16,512]{2,1,0:T(8,128)(2,1)S(1)} all-to-all(bf16[16,16,512]{2,1,0:T(8,128)(2,1)S(1)} %shard_map.60), channel_id=1, replica_groups=mesh['vocab'=32,'hidden'=16] {'hidden'}, dimensions={0} | all-to-all | bytes 524288 | tf_op jit(solution)/shard_map/all_to_all | solution.py:33
  51.0 0.2 shard_map.61
  51.2 9.8 %all_to_all.22.refs_0_ = bf16[8,72,128]{2,1,0:T(8,128)(2,1)S(1)} all-to-all(bf16[8,72,128]{2,1,0:T(8,128)(2,1)S(1)} %shard_map.61), channel_id=1, replica_groups={{0,16,128,144,256,272,384,400},{32,48,160,176,288,304,416,432},{64,80,1..., dimensions={0} | all-to-all | bytes 294912 | tf_op jit(solution)/shard_map/all_to_all | solution.py:33
  61.0 0.7 shard_map.62
  61.7 17.9 %all_to_all.23.refs_0_ = bf16[32,40,128]{2,1,0:T(8,128)(2,1)S(1)} all-to-all(bf16[32,40,128]{2,1,0:T(8,128)(2,1)S(1)} %shard_map.62), channel_id=1, replica_groups=mesh['vocab'=32,'hidden'=16] {'vocab'}, dimensions={0} | all-to-all | bytes 655360 | tf_op jit(solution)/shard_map/all_to_all | solution.py:33
  79.6 0.7 shard_map.63
Async XLA Ops:
  1.9 27.1 %copy-start = (bf16[512,256]{1,0:T(8,128)(2,1)S(1)}, bf16[512,256]{1,0:T(8,128)(2,1)}, u32[]{:S(2)}) copy-start(bf16[512,256]{1,0:T(8,128)(2,1)} %grad_out.1) | copy-start | bytes 786436
  1.9 27.1 %copy-start.1 = (bf16[128,256]{1,0:T(8,128)(2,1)S(1)}, bf16[128,256]{1,0:T(8,128)(2,1)}, u32[]{:S(2)}) copy-start(bf16[128,256]{1,0:T(8,128)(2,1)} %refs_2_.1) | copy-start | bytes 196612

commit v8 on v7

--- a/solution.py
+++ b/solution.py
@@ -76,10 +76,27 @@
         out[peer] = mine
 
 
-def lookup_body(owners, table, places, projection, grad_out, out):
-    width = out.shape[1] // 2
+def split_lanes(value, upper, keep, send):
+    half = value.shape[1] // 2
+    low, high = value[:, :half], value[:, half:]
+    keep[...] = jnp.where(upper, high, low)
+    send[...] = jnp.where(upper, low, high).astype(BF16)
+
+
+def partial_body(projection, grad_out, keep, send):
+    upper = (lax.axis_index("hidden") & 1) == 1
+    split_lanes(contract_last(projection[...], grad_out[...]), upper, keep, send)
+
+
+def pair_body(kept, arrived, keep, send):
+    upper = ((lax.axis_index("hidden") >> 1) & 1) == 1
+    split_lanes(kept[...] + arrived[...].astype(F32), upper, keep, send)
+
+
+def lookup_body(owners, table, places, kept, arrived, out):
+    width = out.shape[1]
     count = places.shape[1]
-    partial = contract_last(projection[...], grad_out[...])
+    partial = kept[...] + arrived[...].astype(F32)
     owner, row = places[0:1, :], places[1:2, :]
     half = width // 2
     lines = table.shape[2]
@@ -105,8 +122,8 @@
     total = jnp.concatenate(sums, axis=0)
     mine = total.astype(BF16)
     for peer in range(out.shape[0]):
-        out[peer, :width] = mine
-        out[peer, width:] = partial[peer * width : (peer + 1) * width].astype(BF16)
+        out[peer, :, :count] = mine
+        out[peer, :, count:] = partial[peer * width : (peer + 1) * width].astype(BF16)
 
 
 def rows_of_lanes(value):
@@ -115,14 +132,16 @@
 
 def products_body(arrived, grad_out, digits, out):
     peers = arrived.shape[0]
-    width = arrived.shape[1] // 2
-    embedded = jnp.concatenate([arrived[p, :width] for p in range(peers)], axis=0)
+    count = grad_out.shape[0]
+    embedded = jnp.concatenate([arrived[p, :, :count] for p in range(peers)], axis=0)
     product = jnp.dot(embedded, grad_out[...], preferred_element_type=F32)
     product = jnp.concatenate(rows_of_lanes(product), axis=0).astype(BF16)
-    grad = arrived[0, width:].astype(F32)
-    for peer in range(1, peers):
-        grad = grad + arrived[peer, width:].astype(F32)
-    small = [part.astype(BF16) for part in [*rows_of_lanes(grad), digits[...]]]
+    grads = []
+    for core in range(2):
+        for chip in range(2):
+            senders = range(2 * chip + core, peers, 4)
+            grads.append(sum(arrived[p, :, count:].astype(F32) for p in senders))
+    small = [part.astype(BF16) for part in [*grads, digits[...]]]
     members = out.shape[0]
     piece = product.shape[0] // members
     for peer in range(members):
@@ -222,14 +241,24 @@
     def last_sums(*refs):
         last_sums_body(piece, *refs)
 
+    def to_partner(send, bit):
+        return lax.ppermute(send, "hidden", [(i, i ^ bit) for i in range(peers)])
+
+    def halves(columns):
+        return (S((depth, columns), F32), S((depth, columns), BF16))
+
+    keep, send = run(
+        partial_body, halves(count // 2), projection, grad_out, flops=2 * depth * count * hidden, limit=4
+    )
+    keep, send = run(pair_body, halves(count // 4), keep, to_partner(send, 1), flops=keep.size, limit=4)
     looked = run(
         lookup,
-        S((peers, 2 * width, count), BF16),
+        S((peers, width, count + count // 4), BF16),
         columns,
         places,
-        projection,
-        grad_out,
-        flops=2 * owners * width * rows * count + 2 * depth * count * hidden,
+        keep,
+        to_partner(send, 2),
+        flops=2 * owners * width * rows * count,
         limit=8,
     )
     looked = exchange(looked, "hidden")

time: 80.5 us -> 79.5 us (0.988)
  blocking collectives: 76.1 us -> 47 us
  starting transfers between devices: 0 us -> 16.5 us
  waiting for transfers between devices: 0 us -> 10.5 us
  Pallas kernels: 3.49 us -> 4.4 us
    all_to_all x4 -> x3, blocking collectives: 76.1 us -> 47 us  [exchange(): lax.all_to_all(blocks, axis, split_axis=0, concat_axis=0, tiled=True, axi...]
    all_to_all x0 -> x1, starting transfers between devices: none -> 10.3 us  [exchange(): lax.all_to_all(blocks, axis, split_axis=0, concat_axis=0, tiled=True, axi...]
    all_to_all x0 -> x1, waiting for transfers between devices: none -> 7.38 us  [exchange(): lax.all_to_all(blocks, axis, split_axis=0, concat_axis=0, tiled=True, axi...]
    ppermute x0 -> x2, starting transfers between devices: none -> 6.2 us  [to_partner(): return lax.ppermute(send, 'hidden', [(i, i ^ bit) for i in range(peers)])]
    ppermute x0 -> x2, waiting for transfers between devices: none -> 3.1 us  [to_partner(): return lax.ppermute(send, 'hidden', [(i, i ^ bit) for i in range(peers)])]
    pallas_call x5 -> x7, Pallas kernels: 3.49 us -> 4.4 us  [run(): pl.pallas_call(body, out_shape=out, in_specs=[pl.BlockSpec(memory_space=s...]
  transfers between devices with their start and end apart: 0 -> 3, of which waited for: 0 -> 3; matrix products, arithmetic and copies ran while one was open for 0% -> 0% of each run, Pallas kernels for 0% -> 0%
where the time goes in v8:
time: 79.5 us; the launch traced here: 79.1 us
  blocking collectives  47 us (59%)
  starting transfers between devices  16.5 us (21%)
  waiting for transfers between devices  10.5 us (13%)
  Pallas kernels  4.4 us (6%)
    all_to_all x3, blocking collectives, exchange(): lax.all_to_all(blocks, axis, split_axis=0, concat_axis=0, tiled=True, axi...  47 us
    all_to_all x1, starting transfers between devices, exchange(): lax.all_to_all(blocks, axis, split_axis=0, concat_axis=0, tiled=True, axi...  10.3 us
    all_to_all x1, waiting for transfers between devices, exchange(): lax.all_to_all(blocks, axis, split_axis=0, concat_axis=0, tiled=True, axi...  7.38 us
    ppermute x2, starting transfers between devices, to_partner(): return lax.ppermute(send, 'hidden', [(i, i ^ bit) for i in range(peers)])  6.2 us
    pallas_call x7, Pallas kernels, run(): pl.pallas_call(body, out_shape=out, in_specs=[pl.BlockSpec(memory_space=s...  4.4 us
    ppermute x2, waiting for transfers between devices, to_partner(): return lax.ppermute(send, 'hidden', [(i, i ^ bit) for i in range(peers)])  3.1 us
  transfers between devices with their start and end apart: 3, of which 3 were waited for; matrix products, arithmetic and copies ran while one was open for 0% of the time, Pallas kernels for 0%

profile of v8, /device:TPU:8, one launch (start us, length us, event | category | flops | bytes accessed | tf_op | source)
XLA Modules:
  0.0 79.1 jit_solution(277868756556587205)
XLA Ops:
  0.6 2.0 %shard_map.59 = (bf16[32,4,1920]{2,1,0:T(4,128)(2,1)}, s32[2,512]{1,0:T(2,128)S(1)}, f32[8,128]{1,0:T(8,128)S(1)}) custom-call(bf16[960,128]{1,0:T(8,128)(2,1)} %table_there.1, s32[4,128]{1,0:T(4,128)} %bitcast.2), custom_call_target="tpu_custom_call" | custom-call | flops 1966080 | bytes 747520 | tf_op jit(solution)/shard_map/pallas_call | solution.py:19
  2.7 0.0 copy-start
  2.7 0.0 copy-start.1
  2.7 10.3 %all-to-all-start = ((bf16[32,4,1920]{2,1,0:T(4,128)(2,1)}), bf16[32,4,1920]{2,1,0:T(4,128)(2,1)S(1)}, u32[]{:S(2)}, u32[]{:S(2)}) async-start(bf16[32,4,1920]{2,1,0:T(4,128)(2,1)} %get-tuple-element.11), calls=%async_computation | async-start | bytes 983040 | tf_op jit(solution)/shard_map/all_to_all | solution.py:33
  13.0 0.0 copy-done
  13.0 0.0 copy-done.1
  13.0 0.2 shard_map.60
  13.2 1.9 %collective-permute-start = (bf16[128,256]{1,0:T(8,128)(2,1)S(1)}, bf16[128,256]{1,0:T(8,128)(2,1)S(1)}, u32[]{:S(2)}, u32[]{:S(2)}) collective-permute-start(bf16[128,256]{1,0:T(8,128)(2,1)S(1)} %get-tuple-element.14), channel_id=1, source_target_pairs={{0,1},{1,0},{2,3},{3,2},{4,5},{5,4},{6,7},{7,6},{8,9},{9,8},{10,11... | collective-permute-start | bytes 196616 | tf_op jit(solution)/shard_map/ppermute | solution.py:245
  15.2 1.2 %collective-permute-done.arrived = bf16[128,256]{1,0:T(8,128)(2,1)S(1)} collective-permute-done((bf16[128,256]{1,0:T(8,128)(2,1)S(1)}, bf16[128,256]{1,0:T(8,128)(2,1)S(1)}, u32[]{:S(2)}, u32[]{:S(2)}) %collective-permute-start) | collective-permute-done | bytes 65568 | tf_op jit(solution)/shard_map/ppermute | solution.py:245
  16.4 4.3 %collective-permute-start.1 = (bf16[128,128]{1,0:T(8,128)(2,1)S(1)}, bf16[128,128]{1,0:T(8,128)(2,1)S(1)}, u32[]{:S(2)}, u32[]{:S(2)}) collective-permute-start(bf16[128,128]{1,0:T(8,128)(2,1)S(1)} %get-tuple-element.16), channel_id=1, source_target_pairs={{0,2},{1,3},{2,0},{3,1},{4,6},{5,7},{6,4},{7,5},{8,10},{9,11},{10,... | collective-permute-start | bytes 98312 | tf_op jit(solution)/shard_map/ppermute | solution.py:245
  20.7 1.9 %collective-permute-done.1.refs_3_ = bf16[128,128]{1,0:T(8,128)(2,1)S(1)} collective-permute-done((bf16[128,128]{1,0:T(8,128)(2,1)S(1)}, bf16[128,128]{1,0:T(8,128)(2,1)S(1)}, u32[]{:S(2)}, u32[]{:S(2)}) %collective-permute-start.1) | collective-permute-done | bytes 32800 | tf_op jit(solution)/shard_map/ppermute | solution.py:245
  22.6 7.4 %all-to-all-done.refs_0_ = bf16[32,4,1920]{2,1,0:T(4,128)(2,1)S(1)} async-done(((bf16[32,4,1920]{2,1,0:T(4,128)(2,1)}), bf16[32,4,1920]{2,1,0:T(4,128)(2,1)S(1)}, u32[]{:S(2)}, u32[]{:S(2)}) %all-to-all-start) | async-done | bytes 491552 | tf_op jit(solution)/shard_map/all_to_all | solution.py:33
  30.0 0.5 shard_map.62
  30.5 19.4 %all_to_all.20.arrived = bf16[16,8,640]{2,1,0:T(8,128)(2,1)S(1)} all-to-all(bf16[16,8,640]{2,1,0:T(8,128)(2,1)S(1)} %shard_map.62), channel_id=1, replica_groups=mesh['vocab'=32,'hidden'=16] {'hidden'}, dimensions={0} | all-to-all | bytes 327680 | tf_op jit(solution)/shard_map/all_to_all | solution.py:33
  49.9 0.2 shard_map.63
  50.1 9.7 %all_to_all.21.refs_0_ = bf16[8,72,128]{2,1,0:T(8,128)(2,1)S(1)} all-to-all(bf16[8,72,128]{2,1,0:T(8,128)(2,1)S(1)} %shard_map.63), channel_id=1, replica_groups={{0,16,128,144,256,272,384,400},{32,48,160,176,288,304,416,432},{64,80,1..., dimensions={0} | all-to-all | bytes 294912 | tf_op jit(solution)/shard_map/all_to_all | solution.py:33
  59.8 0.7 shard_map.64
  60.5 17.9 %all_to_all.22.refs_0_ = bf16[32,40,128]{2,1,0:T(8,128)(2,1)S(1)} all-to-all(bf16[32,40,128]{2,1,0:T(8,128)(2,1)S(1)} %shard_map.64), channel_id=1, replica_groups=mesh['vocab'=32,'hidden'=16] {'vocab'}, dimensions={0} | all-to-all | bytes 655360 | tf_op jit(solution)/shard_map/all_to_all | solution.py:33
  78.4 0.7 shard_map.65
  (1 shorter events, 0.0 us)
Async XLA Ops:
  2.7 10.3 %copy-start = (bf16[512,256]{1,0:T(8,128)(2,1)S(1)}, bf16[512,256]{1,0:T(8,128)(2,1)}, u32[]{:S(2)}) copy-start(bf16[512,256]{1,0:T(8,128)(2,1)} %grad_out.3) | copy-start | bytes 786436
  2.7 10.3 %copy-start.1 = (bf16[128,256]{1,0:T(8,128)(2,1)S(1)}, bf16[128,256]{1,0:T(8,128)(2,1)}, u32[]{:S(2)}) copy-start(bf16[128,256]{1,0:T(8,128)(2,1)} %projection.1) | copy-start | bytes 196612
  2.7 27.3 %all-to-all-start = ((bf16[32,4,1920]{2,1,0:T(4,128)(2,1)}), bf16[32,4,1920]{2,1,0:T(4,128)(2,1)S(1)}, u32[]{:S(2)}, u32[]{:S(2)}) async-start(bf16[32,4,1920]{2,1,0:T(4,128)(2,1)} %get-tuple-element.11), calls=%async_computation | async-start | bytes 983040 | tf_op jit(solution)/shard_map/all_to_all | solution.py:33
  13.2 3.1 %collective-permute-start = (bf16[128,256]{1,0:T(8,128)(2,1)S(1)}, bf16[128,256]{1,0:T(8,128)(2,1)S(1)}, u32[]{:S(2)}, u32[]{:S(2)}) collective-permute-start(bf16[128,256]{1,0:T(8,128)(2,1)S(1)} %get-tuple-element.14), channel_id=1, source_target_pairs={{0,1},{1,0},{2,3},{3,2},{4,5},{5,4},{6,7},{7,6},{8,9},{9,8},{10,11... | collective-permute-start | bytes 196616 | tf_op jit(solution)/shard_map/ppermute | solution.py:245
  16.4 6.2 %collective-permute-start.1 = (bf16[128,128]{1,0:T(8,128)(2,1)S(1)}, bf16[128,128]{1,0:T(8,128)(2,1)S(1)}, u32[]{:S(2)}, u32[]{:S(2)}) collective-permute-start(bf16[128,128]{1,0:T(8,128)(2,1)S(1)} %get-tuple-element.16), channel_id=1, source_target_pairs={{0,2},{1,3},{2,0},{3,1},{4,6},{5,7},{6,4},{7,5},{8,10},{9,11},{10,... | collective-permute-start | bytes 98312 | tf_op jit(solution)/shard_map/ppermute | solution.py:245

commit v9 on v8

--- a/solution.py
+++ b/solution.py
@@ -7,10 +7,11 @@
 
 F32, BF16, I32 = jnp.float32, jnp.bfloat16, jnp.int32
 LANES, SUBLANES = 128, 8
+AT_ONCE = 8
 ALONG_Y = 8
 
 
-def run(body, out, *args, flops, limit, space=pltpu.VMEM, scratch=()):
+def run(body, out, *args, flops, limit, space=pltpu.VMEM, scratch=(), specs=None):
     size = lambda a: a.size * a.dtype.itemsize
     vmem = pl.BlockSpec(memory_space=pltpu.VMEM)
     outs = jax.tree.leaves(out)
@@ -20,7 +21,7 @@
         body,
         out_shape=out,
         in_specs=[pl.BlockSpec(memory_space=space)] * len(args),
-        out_specs=jax.tree.map(lambda _: vmem, out),
+        out_specs=specs or jax.tree.map(lambda _: vmem, out),
         scratch_shapes=scratch,
         compiler_params=pltpu.CompilerParams(vmem_limit_bytes=limit * 2**20),
         cost_estimate=pl.CostEstimate(
@@ -47,22 +48,15 @@
     return owner, token - owner * rows
 
 
-def columns_body(table_there, ids_there, out, places, digits, table, ids, arrivals):
+def columns_body(table_there, ids_there, out, places, digits, table, ids, copied, arrivals):
     copies = [
         pltpu.make_async_copy(table_there, table, arrivals.at[0]),
         pltpu.make_async_copy(ids_there, ids, arrivals.at[1]),
     ]
     for copy in copies:
         copy.start()
-    copies[1].wait()
-    owner, row = owner_and_row(ids[...], table.shape[0])
-    digits[...] = jnp.concatenate([owner * 8 + (row >> 7), row & 127], axis=0).astype(F32)
-    for c in range(ids.shape[0]):
-        at = slice(c * LANES, (c + 1) * LANES)
-        places[0:1, at] = owner[c : c + 1]
-        places[1:2, at] = row[c : c + 1]
     copies[0].wait()
-    width = out.shape[1] * 2
+    width = copied.shape[1] * 2
     first = lax.axis_index("hidden") * width
     shape = (width, table.shape[1])
     lane = lax.broadcasted_iota(I32, shape, 1)
@@ -72,8 +66,24 @@
     mine = jnp.concatenate(
         [mine[:half, :whole], mine[half:, :whole], mine[:half, whole:], mine[half:, whole:]], axis=1
     ).astype(BF16)
-    for peer in range(out.shape[0]):
-        out[peer] = mine
+    at_once = copied.shape[0]
+    for peer in range(at_once):
+        copied[peer] = mine
+    copies[1].wait()
+    owner, row = owner_and_row(ids[...], table.shape[0])
+    digits[...] = jnp.concatenate([owner * 8 + (row >> 7), row & 127], axis=0).astype(F32)
+    for c in range(ids.shape[0]):
+        at = slice(c * LANES, (c + 1) * LANES)
+        places[0:1, at] = owner[c : c + 1]
+        places[1:2, at] = row[c : c + 1]
+    leaving = [
+        pltpu.make_async_copy(copied, out.at[pl.ds(i * at_once, at_once)], arrivals.at[2 + i])
+        for i in range(out.shape[0] // at_once)
+    ]
+    for copy in leaving:
+        copy.start()
+    for copy in leaving:
+        copy.wait()
 
 
 def split_lanes(value, upper, keep, send):
@@ -227,8 +237,10 @@
         scratch=[
             pltpu.VMEM(table.shape, table.dtype),
             pltpu.VMEM(by_lane.shape, I32),
-            pltpu.SemaphoreType.DMA((2,)),
+            pltpu.VMEM((AT_ONCE, width // 2, 2 * rows), BF16),
+            pltpu.SemaphoreType.DMA((2 + owners // AT_ONCE,)),
         ],
+        specs=tuple(pl.BlockSpec(memory_space=place) for place in (pltpu.HBM, pltpu.VMEM, pltpu.VMEM)),
     )
     columns = exchange(columns, "vocab")
 

time: 79.5 us -> 79.5 us (level)
  no operation moved by 1% of the time
where the time goes in v9:
time: 79.5 us; the launch traced here: 79.1 us
  blocking collectives  47 us (59%)
  starting transfers between devices  16.5 us (21%)
  waiting for transfers between devices  10.5 us (13%)
  Pallas kernels  4.42 us (6%)
    all_to_all x3, blocking collectives, exchange(): lax.all_to_all(blocks, axis, split_axis=0, concat_axis=0, tiled=True, axi...  47 us
    all_to_all x1, starting transfers between devices, exchange(): lax.all_to_all(blocks, axis, split_axis=0, concat_axis=0, tiled=True, axi...  10.3 us
    all_to_all x1, waiting for transfers between devices, exchange(): lax.all_to_all(blocks, axis, split_axis=0, concat_axis=0, tiled=True, axi...  7.38 us
    ppermute x2, starting transfers between devices, to_partner(): return lax.ppermute(send, 'hidden', [(i, i ^ bit) for i in range(peers)])  6.2 us
    pallas_call x7, Pallas kernels, run(): pl.pallas_call(body, out_shape=out, in_specs=[pl.BlockSpec(memory_space=s...  4.42 us
    ppermute x2, waiting for transfers between devices, to_partner(): return lax.ppermute(send, 'hidden', [(i, i ^ bit) for i in range(peers)])  3.1 us
  transfers between devices with their start and end apart: 3, of which 3 were waited for; matrix products, arithmetic and copies ran while one was open for 0% of the time, Pallas kernels for 0%

profile of v9, /device:TPU:8, one launch (start us, length us, event | category | flops | bytes accessed | tf_op | source)
XLA Modules:
  0.0 79.1 jit_solution(6508032069618852437)
XLA Ops:
  0.6 2.1 %shard_map.59 = (bf16[32,4,1920]{2,1,0:T(4,128)(2,1)}, s32[2,512]{1,0:T(2,128)S(1)}, f32[8,128]{1,0:T(8,128)S(1)}) custom-call(bf16[960,128]{1,0:T(8,128)(2,1)} %table_there.1, s32[4,128]{1,0:T(4,128)} %bitcast.2), custom_call_target="tpu_custom_call" | custom-call | flops 1966080 | bytes 747520 | tf_op jit(solution)/shard_map/pallas_call | solution.py:20
  2.7 0.0 copy-start
  2.7 0.0 copy-start.1
  2.7 10.3 %all-to-all-start = ((bf16[32,4,1920]{2,1,0:T(4,128)(2,1)}), bf16[32,4,1920]{2,1,0:T(4,128)(2,1)S(1)}, u32[]{:S(2)}, u32[]{:S(2)}) async-start(bf16[32,4,1920]{2,1,0:T(4,128)(2,1)} %get-tuple-element.11), calls=%async_computation | async-start | bytes 983040 | tf_op jit(solution)/shard_map/all_to_all | solution.py:34
  13.0 0.0 copy-done
  13.0 0.0 copy-done.1
  13.1 0.2 shard_map.60
  13.3 1.9 %collective-permute-start = (bf16[128,256]{1,0:T(8,128)(2,1)S(1)}, bf16[128,256]{1,0:T(8,128)(2,1)S(1)}, u32[]{:S(2)}, u32[]{:S(2)}) collective-permute-start(bf16[128,256]{1,0:T(8,128)(2,1)S(1)} %get-tuple-element.14), channel_id=1, source_target_pairs={{0,1},{1,0},{2,3},{3,2},{4,5},{5,4},{6,7},{7,6},{8,9},{9,8},{10,11... | collective-permute-start | bytes 196616 | tf_op jit(solution)/shard_map/ppermute | solution.py:257
  15.2 1.2 %collective-permute-done.arrived = bf16[128,256]{1,0:T(8,128)(2,1)S(1)} collective-permute-done((bf16[128,256]{1,0:T(8,128)(2,1)S(1)}, bf16[128,256]{1,0:T(8,128)(2,1)S(1)}, u32[]{:S(2)}, u32[]{:S(2)}) %collective-permute-start) | collective-permute-done | bytes 65568 | tf_op jit(solution)/shard_map/ppermute | solution.py:257
  16.5 4.3 %collective-permute-start.1 = (bf16[128,128]{1,0:T(8,128)(2,1)S(1)}, bf16[128,128]{1,0:T(8,128)(2,1)S(1)}, u32[]{:S(2)}, u32[]{:S(2)}) collective-permute-start(bf16[128,128]{1,0:T(8,128)(2,1)S(1)} %get-tuple-element.16), channel_id=1, source_target_pairs={{0,2},{1,3},{2,0},{3,1},{4,6},{5,7},{6,4},{7,5},{8,10},{9,11},{10,... | collective-permute-start | bytes 98312 | tf_op jit(solution)/shard_map/ppermute | solution.py:257
  20.7 1.9 %collective-permute-done.1.refs_3_ = bf16[128,128]{1,0:T(8,128)(2,1)S(1)} collective-permute-done((bf16[128,128]{1,0:T(8,128)(2,1)S(1)}, bf16[128,128]{1,0:T(8,128)(2,1)S(1)}, u32[]{:S(2)}, u32[]{:S(2)}) %collective-permute-start.1) | collective-permute-done | bytes 32800 | tf_op jit(solution)/shard_map/ppermute | solution.py:257
  22.6 7.4 %all-to-all-done.refs_0_ = bf16[32,4,1920]{2,1,0:T(4,128)(2,1)S(1)} async-done(((bf16[32,4,1920]{2,1,0:T(4,128)(2,1)}), bf16[32,4,1920]{2,1,0:T(4,128)(2,1)S(1)}, u32[]{:S(2)}, u32[]{:S(2)}) %all-to-all-start) | async-done | bytes 491552 | tf_op jit(solution)/shard_map/all_to_all | solution.py:34
  30.0 0.5 shard_map.62
  30.5 19.4 %all_to_all.20.arrived = bf16[16,8,640]{2,1,0:T(8,128)(2,1)S(1)} all-to-all(bf16[16,8,640]{2,1,0:T(8,128)(2,1)S(1)} %shard_map.62), channel_id=1, replica_groups=mesh['vocab'=32,'hidden'=16] {'hidden'}, dimensions={0} | all-to-all | bytes 327680 | tf_op jit(solution)/shard_map/all_to_all | solution.py:34
  50.0 0.2 shard_map.63
  50.2 9.7 %all_to_all.21.refs_0_ = bf16[8,72,128]{2,1,0:T(8,128)(2,1)S(1)} all-to-all(bf16[8,72,128]{2,1,0:T(8,128)(2,1)S(1)} %shard_map.63), channel_id=1, replica_groups={{0,16,128,144,256,272,384,400},{32,48,160,176,288,304,416,432},{64,80,1..., dimensions={0} | all-to-all | bytes 294912 | tf_op jit(solution)/shard_map/all_to_all | solution.py:34
  59.8 0.7 shard_map.64
  60.6 17.9 %all_to_all.22.refs_0_ = bf16[32,40,128]{2,1,0:T(8,128)(2,1)S(1)} all-to-all(bf16[32,40,128]{2,1,0:T(8,128)(2,1)S(1)} %shard_map.64), channel_id=1, replica_groups=mesh['vocab'=32,'hidden'=16] {'vocab'}, dimensions={0} | all-to-all | bytes 655360 | tf_op jit(solution)/shard_map/all_to_all | solution.py:34
  78.4 0.7 shard_map.65
  (1 shorter events, 0.0 us)
Async XLA Ops:
  2.7 10.3 %copy-start = (bf16[512,256]{1,0:T(8,128)(2,1)S(1)}, bf16[512,256]{1,0:T(8,128)(2,1)}, u32[]{:S(2)}) copy-start(bf16[512,256]{1,0:T(8,128)(2,1)} %grad_out.3) | copy-start | bytes 786436
  2.7 10.3 %copy-start.1 = (bf16[128,256]{1,0:T(8,128)(2,1)S(1)}, bf16[128,256]{1,0:T(8,128)(2,1)}, u32[]{:S(2)}) copy-start(bf16[128,256]{1,0:T(8,128)(2,1)} %projection.1) | copy-start | bytes 196612
  2.7 27.3 %all-to-all-start = ((bf16[32,4,1920]{2,1,0:T(4,128)(2,1)}), bf16[32,4,1920]{2,1,0:T(4,128)(2,1)S(1)}, u32[]{:S(2)}, u32[]{:S(2)}) async-start(bf16[32,4,1920]{2,1,0:T(4,128)(2,1)} %get-tuple-element.11), calls=%async_computation | async-start | bytes 983040 | tf_op jit(solution)/shard_map/all_to_all | solution.py:34
  13.3 3.1 %collective-permute-start = (bf16[128,256]{1,0:T(8,128)(2,1)S(1)}, bf16[128,256]{1,0:T(8,128)(2,1)S(1)}, u32[]{:S(2)}, u32[]{:S(2)}) collective-permute-start(bf16[128,256]{1,0:T(8,128)(2,1)S(1)} %get-tuple-element.14), channel_id=1, source_target_pairs={{0,1},{1,0},{2,3},{3,2},{4,5},{5,4},{6,7},{7,6},{8,9},{9,8},{10,11... | collective-permute-start | bytes 196616 | tf_op jit(solution)/shard_map/ppermute | solution.py:257
  16.5 6.2 %collective-permute-start.1 = (bf16[128,128]{1,0:T(8,128)(2,1)S(1)}, bf16[128,128]{1,0:T(8,128)(2,1)S(1)}, u32[]{:S(2)}, u32[]{:S(2)}) collective-permute-start(bf16[128,128]{1,0:T(8,128)(2,1)S(1)} %get-tuple-element.16), channel_id=1, source_target_pairs={{0,2},{1,3},{2,0},{3,1},{4,6},{5,7},{6,4},{7,5},{8,10},{9,11},{10,... | collective-permute-start | bytes 98312 | tf_op jit(solution)/shard_map/ppermute | solution.py:257

commit v10 on v9

--- a/solution.py
+++ b/solution.py
@@ -41,6 +41,10 @@
 def one_hot_rows(which, rows):
     shape = (rows, which.shape[1])
     return (lax.broadcasted_iota(I32, shape, 0) == which).astype(F32).astype(BF16)
+
+
+def turn(vocab, owners):
+    return (vocab % ALONG_Y) * (owners // ALONG_Y) + vocab // ALONG_Y
 
 
 def owner_and_row(token, rows):
@@ -70,11 +74,12 @@
     for peer in range(at_once):
         copied[peer] = mine
     copies[1].wait()
+    along_x = out.shape[0] // ALONG_Y
     owner, row = owner_and_row(ids[...], table.shape[0])
     digits[...] = jnp.concatenate([owner * 8 + (row >> 7), row & 127], axis=0).astype(F32)
     for c in range(ids.shape[0]):
         at = slice(c * LANES, (c + 1) * LANES)
-        places[0:1, at] = owner[c : c + 1]
+        places[0:1, at] = (owner[c : c + 1] & (ALONG_Y - 1)) * along_x + (owner[c : c + 1] >> 3)
         places[1:2, at] = row[c : c + 1]
     leaving = [
         pltpu.make_async_copy(copied, out.at[pl.ds(i * at_once, at_once)], arrivals.at[2 + i])
@@ -190,8 +195,8 @@
         sums = sums + contract_last(jnp.concatenate(left, axis=1), jnp.concatenate(right, axis=1))
     sums = sums.astype(BF16)
     for v in range(owners):
-        out[v, :piece] = total
-        out[v, piece:] = sums[v * SUBLANES : (v + 1) * SUBLANES]
+        out[turn(v, owners), :piece] = total
+        out[turn(v, owners), piece:] = sums[v * SUBLANES : (v + 1) * SUBLANES]
 
 
 def last_sums_body(piece, arrived, table_grad, projection_grad):
@@ -201,9 +206,9 @@
     members = depth * projection_grad.shape[1] // LANES // piece
     for member in range(members):
         first = (member >> 1) * ALONG_Y + (member & 1)
-        total = arrived[first].astype(F32)
+        total = arrived[turn(first, owners)].astype(F32)
         for peer in range(first + 2, first + ALONG_Y, 2):
-            total = total + arrived[peer].astype(F32)
+            total = total + arrived[turn(peer, owners)].astype(F32)
         at, lane = member * piece % depth, member * piece // depth * LANES
         projection_grad[at : at + piece, lane : lane + LANES] = total[:piece]
         wide = min(LANES, rows - member * LANES)
@@ -217,6 +222,7 @@
     groups = [
         [x * ALONG_Y + y + bit for x in range(along_x) for bit in range(2)] for y in range(0, ALONG_Y, 2)
     ]
+    turned = [sorted(range(owners), key=lambda v: turn(v, owners))]
     rows, depth = table.shape
     width = depth // peers
     count = token_ids.shape[0]
@@ -242,7 +248,7 @@
         ],
         specs=tuple(pl.BlockSpec(memory_space=place) for place in (pltpu.HBM, pltpu.VMEM, pltpu.VMEM)),
     )
-    columns = exchange(columns, "vocab")
+    columns = exchange(columns, "vocab", turned)
 
     def lookup(*refs):
         lookup_body(owners, *refs)
@@ -293,7 +299,7 @@
         flops=2 * members * count * owners * SUBLANES * LANES,
         limit=8,
     )
-    summed = exchange(summed, "vocab")
+    summed = exchange(summed, "vocab", turned)
 
     table_grad, projection_grad = run(
         last_sums, (S((width, rows), F32), S((depth, hidden), F32)), summed, flops=summed.size, limit=8

time: 79.5 us -> 79.5 us (level)
  no operation moved by 1% of the time
where the time goes in v10:
time: 79.5 us; the launch traced here: 79.1 us
  blocking collectives  47.3 us (59%)
  starting transfers between devices  16.5 us (21%)
  waiting for transfers between devices  10.1 us (13%)
  Pallas kernels  4.43 us (6%)
    all_to_all x3, blocking collectives, exchange(): lax.all_to_all(blocks, axis, split_axis=0, concat_axis=0, tiled=True, axi...  47.3 us
    all_to_all x1, starting transfers between devices, exchange(): lax.all_to_all(blocks, axis, split_axis=0, concat_axis=0, tiled=True, axi...  10.3 us
    all_to_all x1, waiting for transfers between devices, exchange(): lax.all_to_all(blocks, axis, split_axis=0, concat_axis=0, tiled=True, axi...  6.96 us
    ppermute x2, starting transfers between devices, to_partner(): return lax.ppermute(send, 'hidden', [(i, i ^ bit) for i in range(peers)])  6.2 us
    pallas_call x7, Pallas kernels, run(): pl.pallas_call(body, out_shape=out, in_specs=[pl.BlockSpec(memory_space=s...  4.43 us
    ppermute x2, waiting for transfers between devices, to_partner(): return lax.ppermute(send, 'hidden', [(i, i ^ bit) for i in range(peers)])  3.1 us
  transfers between devices with their start and end apart: 3, of which 3 were waited for; matrix products, arithmetic and copies ran while one was open for 0% of the time, Pallas kernels for 0%

profile of v10, /device:TPU:8, one launch (start us, length us, event | category | flops | bytes accessed | tf_op | source)
XLA Modules:
  0.0 79.1 jit_solution(6676713470400481070)
XLA Ops:
  0.6 2.1 %shard_map.59 = (bf16[32,4,1920]{2,1,0:T(4,128)(2,1)}, s32[2,512]{1,0:T(2,128)S(1)}, f32[8,128]{1,0:T(8,128)S(1)}) custom-call(bf16[960,128]{1,0:T(8,128)(2,1)} %table_there.1, s32[4,128]{1,0:T(4,128)} %bitcast.2), custom_call_target="tpu_custom_call" | custom-call | flops 1966080 | bytes 747520 | tf_op jit(solution)/shard_map/pallas_call | solution.py:20
  2.7 0.0 copy-start
  2.7 0.0 copy-start.1
  2.7 10.3 %all-to-all-start = ((bf16[32,4,1920]{2,1,0:T(4,128)(2,1)}), bf16[32,4,1920]{2,1,0:T(4,128)(2,1)S(1)}, u32[]{:S(2)}, u32[]{:S(2)}) async-start(bf16[32,4,1920]{2,1,0:T(4,128)(2,1)} %get-tuple-element.11), calls=%async_computation | async-start | bytes 983040 | tf_op jit(solution)/shard_map/all_to_all | solution.py:34
  13.0 0.0 copy-done
  13.0 0.0 copy-done.1
  13.1 0.2 shard_map.60
  13.3 1.9 %collective-permute-start = (bf16[128,256]{1,0:T(8,128)(2,1)S(1)}, bf16[128,256]{1,0:T(8,128)(2,1)S(1)}, u32[]{:S(2)}, u32[]{:S(2)}) collective-permute-start(bf16[128,256]{1,0:T(8,128)(2,1)S(1)} %get-tuple-element.14), channel_id=1, source_target_pairs={{0,1},{1,0},{2,3},{3,2},{4,5},{5,4},{6,7},{7,6},{8,9},{9,8},{10,11... | collective-permute-start | bytes 196616 | tf_op jit(solution)/shard_map/ppermute | solution.py:263
  15.2 1.2 %collective-permute-done.arrived = bf16[128,256]{1,0:T(8,128)(2,1)S(1)} collective-permute-done((bf16[128,256]{1,0:T(8,128)(2,1)S(1)}, bf16[128,256]{1,0:T(8,128)(2,1)S(1)}, u32[]{:S(2)}, u32[]{:S(2)}) %collective-permute-start) | collective-permute-done | bytes 65568 | tf_op jit(solution)/shard_map/ppermute | solution.py:263
  16.5 4.3 %collective-permute-start.1 = (bf16[128,128]{1,0:T(8,128)(2,1)S(1)}, bf16[128,128]{1,0:T(8,128)(2,1)S(1)}, u32[]{:S(2)}, u32[]{:S(2)}) collective-permute-start(bf16[128,128]{1,0:T(8,128)(2,1)S(1)} %get-tuple-element.16), channel_id=1, source_target_pairs={{0,2},{1,3},{2,0},{3,1},{4,6},{5,7},{6,4},{7,5},{8,10},{9,11},{10,... | collective-permute-start | bytes 98312 | tf_op jit(solution)/shard_map/ppermute | solution.py:263
  20.7 1.9 %collective-permute-done.1.refs_3_ = bf16[128,128]{1,0:T(8,128)(2,1)S(1)} collective-permute-done((bf16[128,128]{1,0:T(8,128)(2,1)S(1)}, bf16[128,128]{1,0:T(8,128)(2,1)S(1)}, u32[]{:S(2)}, u32[]{:S(2)}) %collective-permute-start.1) | collective-permute-done | bytes 32800 | tf_op jit(solution)/shard_map/ppermute | solution.py:263
  22.6 7.0 %all-to-all-done.refs_0_ = bf16[32,4,1920]{2,1,0:T(4,128)(2,1)S(1)} async-done(((bf16[32,4,1920]{2,1,0:T(4,128)(2,1)}), bf16[32,4,1920]{2,1,0:T(4,128)(2,1)S(1)}, u32[]{:S(2)}, u32[]{:S(2)}) %all-to-all-start) | async-done | bytes 491552 | tf_op jit(solution)/shard_map/all_to_all | solution.py:34
  29.6 0.5 shard_map.62
  30.1 19.4 %all_to_all.20.arrived = bf16[16,8,640]{2,1,0:T(8,128)(2,1)S(1)} all-to-all(bf16[16,8,640]{2,1,0:T(8,128)(2,1)S(1)} %shard_map.62), channel_id=1, replica_groups=mesh['vocab'=32,'hidden'=16] {'hidden'}, dimensions={0} | all-to-all | bytes 327680 | tf_op jit(solution)/shard_map/all_to_all | solution.py:34
  49.5 0.2 shard_map.63
  49.7 10.0 %all_to_all.21.refs_0_ = bf16[8,72,128]{2,1,0:T(8,128)(2,1)S(1)} all-to-all(bf16[8,72,128]{2,1,0:T(8,128)(2,1)S(1)} %shard_map.63), channel_id=1, replica_groups={{0,16,128,144,256,272,384,400},{32,48,160,176,288,304,416,432},{64,80,1..., dimensions={0} | all-to-all | bytes 294912 | tf_op jit(solution)/shard_map/all_to_all | solution.py:34
  59.7 0.7 shard_map.64
  60.4 17.9 %all_to_all.22.refs_0_ = bf16[32,40,128]{2,1,0:T(8,128)(2,1)S(1)} all-to-all(bf16[32,40,128]{2,1,0:T(8,128)(2,1)S(1)} %shard_map.64), channel_id=1, replica_groups={{0,128,256,384,16,144,272,400,32,160,288,416,48,176,304,432,64,192,320,..., dimensions={0} | all-to-all | bytes 655360 | tf_op jit(solution)/shard_map/all_to_all | solution.py:34
  78.4 0.7 shard_map.65
  (1 shorter events, 0.0 us)
Async XLA Ops:
  2.7 10.3 %copy-start = (bf16[512,256]{1,0:T(8,128)(2,1)S(1)}, bf16[512,256]{1,0:T(8,128)(2,1)}, u32[]{:S(2)}) copy-start(bf16[512,256]{1,0:T(8,128)(2,1)} %grad_out.3) | copy-start | bytes 786436
  2.7 10.3 %copy-start.1 = (bf16[128,256]{1,0:T(8,128)(2,1)S(1)}, bf16[128,256]{1,0:T(8,128)(2,1)}, u32[]{:S(2)}) copy-start(bf16[128,256]{1,0:T(8,128)(2,1)} %projection.1) | copy-start | bytes 196612
  2.7 26.9 %all-to-all-start = ((bf16[32,4,1920]{2,1,0:T(4,128)(2,1)}), bf16[32,4,1920]{2,1,0:T(4,128)(2,1)S(1)}, u32[]{:S(2)}, u32[]{:S(2)}) async-start(bf16[32,4,1920]{2,1,0:T(4,128)(2,1)} %get-tuple-element.11), calls=%async_computation | async-start | bytes 983040 | tf_op jit(solution)/shard_map/all_to_all | solution.py:34
  13.3 3.1 %collective-permute-start = (bf16[128,256]{1,0:T(8,128)(2,1)S(1)}, bf16[128,256]{1,0:T(8,128)(2,1)S(1)}, u32[]{:S(2)}, u32[]{:S(2)}) collective-permute-start(bf16[128,256]{1,0:T(8,128)(2,1)S(1)} %get-tuple-element.14), channel_id=1, source_target_pairs={{0,1},{1,0},{2,3},{3,2},{4,5},{5,4},{6,7},{7,6},{8,9},{9,8},{10,11... | collective-permute-start | bytes 196616 | tf_op jit(solution)/shard_map/ppermute | solution.py:263
  16.5 6.2 %collective-permute-start.1 = (bf16[128,128]{1,0:T(8,128)(2,1)S(1)}, bf16[128,128]{1,0:T(8,128)(2,1)S(1)}, u32[]{:S(2)}, u32[]{:S(2)}) collective-permute-start(bf16[128,128]{1,0:T(8,128)(2,1)S(1)} %get-tuple-element.16), channel_id=1, source_target_pairs={{0,2},{1,3},{2,0},{3,1},{4,6},{5,7},{6,4},{7,5},{8,10},{9,11},{10,... | collective-permute-start | bytes 98312 | tf_op jit(solution)/shard_map/ppermute | solution.py:263

commit v11 on v8

--- a/solution.py
+++ b/solution.py
@@ -47,21 +47,10 @@
     return owner, token - owner * rows
 
 
-def columns_body(table_there, ids_there, out, places, digits, table, ids, arrivals):
-    copies = [
-        pltpu.make_async_copy(table_there, table, arrivals.at[0]),
-        pltpu.make_async_copy(ids_there, ids, arrivals.at[1]),
-    ]
-    for copy in copies:
-        copy.start()
-    copies[1].wait()
-    owner, row = owner_and_row(ids[...], table.shape[0])
-    digits[...] = jnp.concatenate([owner * 8 + (row >> 7), row & 127], axis=0).astype(F32)
-    for c in range(ids.shape[0]):
-        at = slice(c * LANES, (c + 1) * LANES)
-        places[0:1, at] = owner[c : c + 1]
-        places[1:2, at] = row[c : c + 1]
-    copies[0].wait()
+def columns_body(table_there, out, table, arrival):
+    copy = pltpu.make_async_copy(table_there, table, arrival.at[0])
+    copy.start()
+    copy.wait()
     width = out.shape[1] * 2
     first = lax.axis_index("hidden") * width
     shape = (width, table.shape[1])
@@ -83,7 +72,13 @@
     send[...] = jnp.where(upper, low, high).astype(BF16)
 
 
-def partial_body(projection, grad_out, keep, send):
+def partial_body(rows, projection, grad_out, ids, keep, send, places, digits):
+    owner, row = owner_and_row(ids[...], rows)
+    digits[...] = jnp.concatenate([owner * 8 + (row >> 7), row & 127], axis=0).astype(F32)
+    for c in range(ids.shape[0]):
+        at = slice(c * LANES, (c + 1) * LANES)
+        places[0:1, at] = owner[c : c + 1]
+        places[1:2, at] = row[c : c + 1]
     upper = (lax.axis_index("hidden") & 1) == 1
     split_lanes(contract_last(projection[...], grad_out[...]), upper, keep, send)
 
@@ -108,10 +103,11 @@
     rest = held[:, 2 * whole :]
     left = row - whole
     right = jnp.where(left >= 0, left + (rows - whole), -1)
-    tails = [one_hot_rows(left, LANES // 2), one_hot_rows(right, LANES)]
-    tails[0] = jnp.concatenate([tails[0], jnp.zeros_like(tails[0])], axis=0)
-    first = every[: owners * half] + jnp.dot(rest, tails[0], preferred_element_type=F32)
-    other = every[owners * half :] + jnp.dot(rest, tails[1], preferred_element_type=F32)
+    left = jnp.where(left < rows - whole, left, -1)
+    tails = jnp.concatenate([one_hot_rows(left, LANES), one_hot_rows(right, LANES)], axis=1)
+    ends = jnp.dot(rest, tails, preferred_element_type=F32)
+    first = every[: owners * half] + ends[:, :count]
+    other = every[owners * half :] + ends[:, count:]
     pair = owner - (lax.broadcasted_iota(I32, (width, count), 0) >= half).astype(I32)
     sums = []
     for found in (first, other):
@@ -215,20 +211,14 @@
     chunks = count // LANES
     S = jax.ShapeDtypeStruct
 
-    by_lane = token_ids.reshape(chunks, LANES)
-    columns, places, digits = run(
+    columns = run(
         columns_body,
-        (S((owners, width // 2, 2 * rows), BF16), S((2, count), I32), S((2 * chunks, LANES), F32)),
+        S((owners, width // 2, 2 * rows), BF16),
         table,
-        by_lane,
         flops=2 * depth * rows * width,
         limit=4,
         space=pltpu.HBM,
-        scratch=[
-            pltpu.VMEM(table.shape, table.dtype),
-            pltpu.VMEM(by_lane.shape, I32),
-            pltpu.SemaphoreType.DMA((2,)),
-        ],
+        scratch=[pltpu.VMEM(table.shape, table.dtype), pltpu.SemaphoreType.DMA((1,))],
     )
     columns = exchange(columns, "vocab")
 
@@ -247,8 +237,17 @@
     def halves(columns):
         return (S((depth, columns), F32), S((depth, columns), BF16))
 
-    keep, send = run(
-        partial_body, halves(count // 2), projection, grad_out, flops=2 * depth * count * hidden, limit=4
+    def partial(*refs):
+        partial_body(rows, *refs)
+
+    keep, send, places, digits = run(
+        partial,
+        (*halves(count // 2), S((2, count), I32), S((2 * chunks, LANES), F32)),
+        projection,
+        grad_out,
+        token_ids.reshape(chunks, LANES),
+        flops=2 * depth * count * hidden,
+        limit=4,
     )
     keep, send = run(pair_body, halves(count // 4), keep, to_partner(send, 1), flops=keep.size, limit=4)
     looked = run(

time: 79.5 us -> 79.5 us (level)
  no operation moved by 1% of the time
where the time goes in v11:
time: 79.5 us; the launch traced here: 79.1 us
  blocking collectives  47 us (59%)
  starting transfers between devices  16.5 us (21%)
  waiting for transfers between devices  10.5 us (13%)
  Pallas kernels  4.39 us (6%)
    all_to_all x3, blocking collectives, exchange(): lax.all_to_all(blocks, axis, split_axis=0, concat_axis=0, tiled=True, axi...  47 us
    all_to_all x1, starting transfers between devices, exchange(): lax.all_to_all(blocks, axis, split_axis=0, concat_axis=0, tiled=True, axi...  10.3 us
    all_to_all x1, waiting for transfers between devices, exchange(): lax.all_to_all(blocks, axis, split_axis=0, concat_axis=0, tiled=True, axi...  7.37 us
    ppermute x2, starting transfers between devices, to_partner(): return lax.ppermute(send, 'hidden', [(i, i ^ bit) for i in range(peers)])  6.2 us
    pallas_call x7, Pallas kernels, run(): pl.pallas_call(body, out_shape=out, in_specs=[pl.BlockSpec(memory_space=s...  4.39 us
    ppermute x2, waiting for transfers between devices, to_partner(): return lax.ppermute(send, 'hidden', [(i, i ^ bit) for i in range(peers)])  3.1 us
  transfers between devices with their start and end apart: 3, of which 3 were waited for; matrix products, arithmetic and copies ran while one was open for 0% of the time, Pallas kernels for 0%

profile of v11, /device:TPU:8, one launch (start us, length us, event | category | flops | bytes accessed | tf_op | source)
XLA Modules:
  0.0 79.1 jit_solution(9170131146229865381)
XLA Ops:
  0.6 2.0 %shard_map.59 = bf16[32,4,1920]{2,1,0:T(4,128)(2,1)} custom-call(bf16[960,128]{1,0:T(8,128)(2,1)} %table_there.1), custom_call_target="tpu_custom_call" | custom-call | flops 1966080 | bytes 737280 | tf_op jit(solution)/shard_map/pallas_call | solution.py:19
  2.6 0.0 copy-start
  2.7 0.0 copy-start.1
  2.7 0.0 copy-start.2
  2.7 10.3 %all-to-all-start = ((bf16[32,4,1920]{2,1,0:T(4,128)(2,1)}), bf16[32,4,1920]{2,1,0:T(4,128)(2,1)S(1)}, u32[]{:S(2)}, u32[]{:S(2)}) async-start(bf16[32,4,1920]{2,1,0:T(4,128)(2,1)} %shard_map.59), calls=%async_computation | async-start | bytes 983040 | tf_op jit(solution)/shard_map/all_to_all | solution.py:33
  13.0 0.0 copy-done
  13.0 0.0 copy-done.1
  13.0 0.0 copy-done.2
  13.0 0.2 shard_map.60
  13.3 1.9 %collective-permute-start = (bf16[128,256]{1,0:T(8,128)(2,1)S(1)}, bf16[128,256]{1,0:T(8,128)(2,1)S(1)}, u32[]{:S(2)}, u32[]{:S(2)}) collective-permute-start(bf16[128,256]{1,0:T(8,128)(2,1)S(1)} %get-tuple-element.12), channel_id=1, source_target_pairs={{0,1},{1,0},{2,3},{3,2},{4,5},{5,4},{6,7},{7,6},{8,9},{9,8},{10,11... | collective-permute-start | bytes 196616 | tf_op jit(solution)/shard_map/ppermute | solution.py:235
  15.2 1.2 %collective-permute-done.arrived = bf16[128,256]{1,0:T(8,128)(2,1)S(1)} collective-permute-done((bf16[128,256]{1,0:T(8,128)(2,1)S(1)}, bf16[128,256]{1,0:T(8,128)(2,1)S(1)}, u32[]{:S(2)}, u32[]{:S(2)}) %collective-permute-start) | collective-permute-done | bytes 65568 | tf_op jit(solution)/shard_map/ppermute | solution.py:235
  16.4 4.3 %collective-permute-start.1 = (bf16[128,128]{1,0:T(8,128)(2,1)S(1)}, bf16[128,128]{1,0:T(8,128)(2,1)S(1)}, u32[]{:S(2)}, u32[]{:S(2)}) collective-permute-start(bf16[128,128]{1,0:T(8,128)(2,1)S(1)} %get-tuple-element.14), channel_id=1, source_target_pairs={{0,2},{1,3},{2,0},{3,1},{4,6},{5,7},{6,4},{7,5},{8,10},{9,11},{10,... | collective-permute-start | bytes 98312 | tf_op jit(solution)/shard_map/ppermute | solution.py:235
  20.7 1.9 %collective-permute-done.1.refs_3_ = bf16[128,128]{1,0:T(8,128)(2,1)S(1)} collective-permute-done((bf16[128,128]{1,0:T(8,128)(2,1)S(1)}, bf16[128,128]{1,0:T(8,128)(2,1)S(1)}, u32[]{:S(2)}, u32[]{:S(2)}) %collective-permute-start.1) | collective-permute-done | bytes 32800 | tf_op jit(solution)/shard_map/ppermute | solution.py:235
  22.6 7.4 %all-to-all-done.refs_0_ = bf16[32,4,1920]{2,1,0:T(4,128)(2,1)S(1)} async-done(((bf16[32,4,1920]{2,1,0:T(4,128)(2,1)}), bf16[32,4,1920]{2,1,0:T(4,128)(2,1)S(1)}, u32[]{:S(2)}, u32[]{:S(2)}) %all-to-all-start) | async-done | bytes 491552 | tf_op jit(solution)/shard_map/all_to_all | solution.py:33
  30.0 0.5 shard_map.62
  30.5 19.4 %all_to_all.20.arrived = bf16[16,8,640]{2,1,0:T(8,128)(2,1)S(1)} all-to-all(bf16[16,8,640]{2,1,0:T(8,128)(2,1)S(1)} %shard_map.62), channel_id=1, replica_groups=mesh['vocab'=32,'hidden'=16] {'hidden'}, dimensions={0} | all-to-all | bytes 327680 | tf_op jit(solution)/shard_map/all_to_all | solution.py:33
  49.9 0.2 shard_map.63
  50.1 9.7 %all_to_all.21.refs_0_ = bf16[8,72,128]{2,1,0:T(8,128)(2,1)S(1)} all-to-all(bf16[8,72,128]{2,1,0:T(8,128)(2,1)S(1)} %shard_map.63), channel_id=1, replica_groups={{0,16,128,144,256,272,384,400},{32,48,160,176,288,304,416,432},{64,80,1..., dimensions={0} | all-to-all | bytes 294912 | tf_op jit(solution)/shard_map/all_to_all | solution.py:33
  59.8 0.7 shard_map.64
  60.5 17.9 %all_to_all.22.refs_0_ = bf16[32,40,128]{2,1,0:T(8,128)(2,1)S(1)} all-to-all(bf16[32,40,128]{2,1,0:T(8,128)(2,1)S(1)} %shard_map.64), channel_id=1, replica_groups=mesh['vocab'=32,'hidden'=16] {'vocab'}, dimensions={0} | all-to-all | bytes 655360 | tf_op jit(solution)/shard_map/all_to_all | solution.py:33
  78.4 0.7 shard_map.65
  (1 shorter events, 0.0 us)
Async XLA Ops:
  2.6 10.4 %copy-start = (bf16[512,256]{1,0:T(8,128)(2,1)S(1)}, bf16[512,256]{1,0:T(8,128)(2,1)}, u32[]{:S(2)}) copy-start(bf16[512,256]{1,0:T(8,128)(2,1)} %grad_out.1) | copy-start | bytes 786436
  2.7 10.4 %copy-start.1 = (bf16[128,256]{1,0:T(8,128)(2,1)S(1)}, bf16[128,256]{1,0:T(8,128)(2,1)}, u32[]{:S(2)}) copy-start(bf16[128,256]{1,0:T(8,128)(2,1)} %refs_0_.1) | copy-start | bytes 196612
  2.7 10.3 %copy-start.2 = (s32[512]{0:T(512)S(1)}, s32[512]{0:T(512)}, u32[]{:S(2)}) copy-start(s32[512]{0:T(512)} %param.4) | copy-start | bytes 6148
  2.7 27.3 %all-to-all-start = ((bf16[32,4,1920]{2,1,0:T(4,128)(2,1)}), bf16[32,4,1920]{2,1,0:T(4,128)(2,1)S(1)}, u32[]{:S(2)}, u32[]{:S(2)}) async-start(bf16[32,4,1920]{2,1,0:T(4,128)(2,1)} %shard_map.59), calls=%async_computation | async-start | bytes 983040 | tf_op jit(solution)/shard_map/all_to_all | solution.py:33
  13.3 3.1 %collective-permute-start = (bf16[128,256]{1,0:T(8,128)(2,1)S(1)}, bf16[128,256]{1,0:T(8,128)(2,1)S(1)}, u32[]{:S(2)}, u32[]{:S(2)}) collective-permute-start(bf16[128,256]{1,0:T(8,128)(2,1)S(1)} %get-tuple-element.12), channel_id=1, source_target_pairs={{0,1},{1,0},{2,3},{3,2},{4,5},{5,4},{6,7},{7,6},{8,9},{9,8},{10,11... | collective-permute-start | bytes 196616 | tf_op jit(solution)/shard_map/ppermute | solution.py:235
  16.4 6.2 %collective-permute-start.1 = (bf16[128,128]{1,0:T(8,128)(2,1)S(1)}, bf16[128,128]{1,0:T(8,128)(2,1)S(1)}, u32[]{:S(2)}, u32[]{:S(2)}) collective-permute-start(bf16[128,128]{1,0:T(8,128)(2,1)S(1)} %get-tuple-element.14), channel_id=1, source_target_pairs={{0,2},{1,3},{2,0},{3,1},{4,6},{5,7},{6,4},{7,5},{8,10},{9,11},{10,... | collective-permute-start | bytes 98312 | tf_op jit(solution)/shard_map/ppermute | solution.py:235

commit v12 on v9

--- a/solution.py
+++ b/solution.py
@@ -7,7 +7,7 @@
 
 F32, BF16, I32 = jnp.float32, jnp.bfloat16, jnp.int32
 LANES, SUBLANES = 128, 8
-AT_ONCE = 8
+AT_ONCE = 2
 ALONG_Y = 8
 
 

time: 79.5 us -> 79.6 us (level)
  no operation moved by 1% of the time
where the time goes in v12:
time: 79.6 us; the launch traced here: 79.2 us
  blocking collectives  47 us (59%)
  starting transfers between devices  16.5 us (21%)
  waiting for transfers between devices  10.5 us (13%)
  Pallas kernels  4.53 us (6%)
    all_to_all x3, blocking collectives, exchange(): lax.all_to_all(blocks, axis, split_axis=0, concat_axis=0, tiled=True, axi...  47 us
    all_to_all x1, starting transfers between devices, exchange(): lax.all_to_all(blocks, axis, split_axis=0, concat_axis=0, tiled=True, axi...  10.3 us
    all_to_all x1, waiting for transfers between devices, exchange(): lax.all_to_all(blocks, axis, split_axis=0, concat_axis=0, tiled=True, axi...  7.38 us
    ppermute x2, starting transfers between devices, to_partner(): return lax.ppermute(send, 'hidden', [(i, i ^ bit) for i in range(peers)])  6.2 us
    pallas_call x7, Pallas kernels, run(): pl.pallas_call(body, out_shape=out, in_specs=[pl.BlockSpec(memory_space=s...  4.53 us
    ppermute x2, waiting for transfers between devices, to_partner(): return lax.ppermute(send, 'hidden', [(i, i ^ bit) for i in range(peers)])  3.1 us
  transfers between devices with their start and end apart: 3, of which 3 were waited for; matrix products, arithmetic and copies ran while one was open for 0% of the time, Pallas kernels for 0%

profile of v12, /device:TPU:8, one launch (start us, length us, event | category | flops | bytes accessed | tf_op | source)
XLA Modules:
  0.0 79.2 jit_solution(5051230072425219046)
XLA Ops:
  0.6 2.2 %shard_map.59 = (bf16[32,4,1920]{2,1,0:T(4,128)(2,1)}, s32[2,512]{1,0:T(2,128)S(1)}, f32[8,128]{1,0:T(8,128)S(1)}) custom-call(bf16[960,128]{1,0:T(8,128)(2,1)} %table_there.1, s32[4,128]{1,0:T(4,128)} %bitcast.2), custom_call_target="tpu_custom_call" | custom-call | flops 1966080 | bytes 747520 | tf_op jit(solution)/shard_map/pallas_call | solution.py:20
  2.8 0.0 copy-start
  2.8 0.0 copy-start.1
  2.8 10.3 %all-to-all-start = ((bf16[32,4,1920]{2,1,0:T(4,128)(2,1)}), bf16[32,4,1920]{2,1,0:T(4,128)(2,1)S(1)}, u32[]{:S(2)}, u32[]{:S(2)}) async-start(bf16[32,4,1920]{2,1,0:T(4,128)(2,1)} %get-tuple-element.11), calls=%async_computation | async-start | bytes 983040 | tf_op jit(solution)/shard_map/all_to_all | solution.py:34
  13.1 0.0 copy-done
  13.1 0.0 copy-done.1
  13.2 0.2 shard_map.60
  13.4 1.9 %collective-permute-start = (bf16[128,256]{1,0:T(8,128)(2,1)S(1)}, bf16[128,256]{1,0:T(8,128)(2,1)S(1)}, u32[]{:S(2)}, u32[]{:S(2)}) collective-permute-start(bf16[128,256]{1,0:T(8,128)(2,1)S(1)} %get-tuple-element.14), channel_id=1, source_target_pairs={{0,1},{1,0},{2,3},{3,2},{4,5},{5,4},{6,7},{7,6},{8,9},{9,8},{10,11... | collective-permute-start | bytes 196616 | tf_op jit(solution)/shard_map/ppermute | solution.py:257
  15.3 1.2 %collective-permute-done.arrived = bf16[128,256]{1,0:T(8,128)(2,1)S(1)} collective-permute-done((bf16[128,256]{1,0:T(8,128)(2,1)S(1)}, bf16[128,256]{1,0:T(8,128)(2,1)S(1)}, u32[]{:S(2)}, u32[]{:S(2)}) %collective-permute-start) | collective-permute-done | bytes 65568 | tf_op jit(solution)/shard_map/ppermute | solution.py:257
  16.6 4.3 %collective-permute-start.1 = (bf16[128,128]{1,0:T(8,128)(2,1)S(1)}, bf16[128,128]{1,0:T(8,128)(2,1)S(1)}, u32[]{:S(2)}, u32[]{:S(2)}) collective-permute-start(bf16[128,128]{1,0:T(8,128)(2,1)S(1)} %get-tuple-element.16), channel_id=1, source_target_pairs={{0,2},{1,3},{2,0},{3,1},{4,6},{5,7},{6,4},{7,5},{8,10},{9,11},{10,... | collective-permute-start | bytes 98312 | tf_op jit(solution)/shard_map/ppermute | solution.py:257
  20.8 1.9 %collective-permute-done.1.refs_3_ = bf16[128,128]{1,0:T(8,128)(2,1)S(1)} collective-permute-done((bf16[128,128]{1,0:T(8,128)(2,1)S(1)}, bf16[128,128]{1,0:T(8,128)(2,1)S(1)}, u32[]{:S(2)}, u32[]{:S(2)}) %collective-permute-start.1) | collective-permute-done | bytes 32800 | tf_op jit(solution)/shard_map/ppermute | solution.py:257
  22.7 7.4 %all-to-all-done.refs_0_ = bf16[32,4,1920]{2,1,0:T(4,128)(2,1)S(1)} async-done(((bf16[32,4,1920]{2,1,0:T(4,128)(2,1)}), bf16[32,4,1920]{2,1,0:T(4,128)(2,1)S(1)}, u32[]{:S(2)}, u32[]{:S(2)}) %all-to-all-start) | async-done | bytes 491552 | tf_op jit(solution)/shard_map/all_to_all | solution.py:34
  30.1 0.5 shard_map.62
  30.6 19.4 %all_to_all.20.arrived = bf16[16,8,640]{2,1,0:T(8,128)(2,1)S(1)} all-to-all(bf16[16,8,640]{2,1,0:T(8,128)(2,1)S(1)} %shard_map.62), channel_id=1, replica_groups=mesh['vocab'=32,'hidden'=16] {'hidden'}, dimensions={0} | all-to-all | bytes 327680 | tf_op jit(solution)/shard_map/all_to_all | solution.py:34
  50.1 0.2 shard_map.63
  50.3 9.7 %all_to_all.21.refs_0_ = bf16[8,72,128]{2,1,0:T(8,128)(2,1)S(1)} all-to-all(bf16[8,72,128]{2,1,0:T(8,128)(2,1)S(1)} %shard_map.63), channel_id=1, replica_groups={{0,16,128,144,256,272,384,400},{32,48,160,176,288,304,416,432},{64,80,1..., dimensions={0} | all-to-all | bytes 294912 | tf_op jit(solution)/shard_map/all_to_all | solution.py:34
  60.0 0.7 shard_map.64
  60.7 17.9 %all_to_all.22.refs_0_ = bf16[32,40,128]{2,1,0:T(8,128)(2,1)S(1)} all-to-all(bf16[32,40,128]{2,1,0:T(8,128)(2,1)S(1)} %shard_map.64), channel_id=1, replica_groups=mesh['vocab'=32,'hidden'=16] {'vocab'}, dimensions={0} | all-to-all | bytes 655360 | tf_op jit(solution)/shard_map/all_to_all | solution.py:34
  78.5 0.7 shard_map.65
  (1 shorter events, 0.0 us)
Async XLA Ops:
  2.8 10.3 %copy-start = (bf16[512,256]{1,0:T(8,128)(2,1)S(1)}, bf16[512,256]{1,0:T(8,128)(2,1)}, u32[]{:S(2)}) copy-start(bf16[512,256]{1,0:T(8,128)(2,1)} %grad_out.3) | copy-start | bytes 786436
  2.8 10.3 %copy-start.1 = (bf16[128,256]{1,0:T(8,128)(2,1)S(1)}, bf16[128,256]{1,0:T(8,128)(2,1)}, u32[]{:S(2)}) copy-start(bf16[128,256]{1,0:T(8,128)(2,1)} %projection.1) | copy-start | bytes 196612
  2.8 27.3 %all-to-all-start = ((bf16[32,4,1920]{2,1,0:T(4,128)(2,1)}), bf16[32,4,1920]{2,1,0:T(4,128)(2,1)S(1)}, u32[]{:S(2)}, u32[]{:S(2)}) async-start(bf16[32,4,1920]{2,1,0:T(4,128)(2,1)} %get-tuple-element.11), calls=%async_computation | async-start | bytes 983040 | tf_op jit(solution)/shard_map/all_to_all | solution.py:34
  13.4 3.1 %collective-permute-start = (bf16[128,256]{1,0:T(8,128)(2,1)S(1)}, bf16[128,256]{1,0:T(8,128)(2,1)S(1)}, u32[]{:S(2)}, u32[]{:S(2)}) collective-permute-start(bf16[128,256]{1,0:T(8,128)(2,1)S(1)} %get-tuple-element.14), channel_id=1, source_target_pairs={{0,1},{1,0},{2,3},{3,2},{4,5},{5,4},{6,7},{7,6},{8,9},{9,8},{10,11... | collective-permute-start | bytes 196616 | tf_op jit(solution)/shard_map/ppermute | solution.py:257
  16.6 6.2 %collective-permute-start.1 = (bf16[128,128]{1,0:T(8,128)(2,1)S(1)}, bf16[128,128]{1,0:T(8,128)(2,1)S(1)}, u32[]{:S(2)}, u32[]{:S(2)}) collective-permute-start(bf16[128,128]{1,0:T(8,128)(2,1)S(1)} %get-tuple-element.16), channel_id=1, source_target_pairs={{0,2},{1,3},{2,0},{3,1},{4,6},{5,7},{6,4},{7,5},{8,10},{9,11},{10,... | collective-permute-start | bytes 98312 | tf_op jit(solution)/shard_map/ppermute | solution.py:257

commit v13 on v12

--- a/solution.py
+++ b/solution.py
@@ -7,7 +7,7 @@
 
 F32, BF16, I32 = jnp.float32, jnp.bfloat16, jnp.int32
 LANES, SUBLANES = 128, 8
-AT_ONCE = 2
+AT_ONCE = 16
 ALONG_Y = 8
 
 

time: 79.6 us -> 79.5 us (level)
  no operation moved by 1% of the time
where the time goes in v13:
time: 79.5 us; the launch traced here: 79.1 us
  blocking collectives  47 us (59%)
  starting transfers between devices  16.5 us (21%)
  waiting for transfers between devices  10.5 us (13%)
  Pallas kernels  4.4 us (6%)
    all_to_all x3, blocking collectives, exchange(): lax.all_to_all(blocks, axis, split_axis=0, concat_axis=0, tiled=True, axi...  47 us
    all_to_all x1, starting transfers between devices, exchange(): lax.all_to_all(blocks, axis, split_axis=0, concat_axis=0, tiled=True, axi...  10.3 us
    all_to_all x1, waiting for transfers between devices, exchange(): lax.all_to_all(blocks, axis, split_axis=0, concat_axis=0, tiled=True, axi...  7.38 us
    ppermute x2, starting transfers between devices, to_partner(): return lax.ppermute(send, 'hidden', [(i, i ^ bit) for i in range(peers)])  6.2 us
    pallas_call x7, Pallas kernels, run(): pl.pallas_call(body, out_shape=out, in_specs=[pl.BlockSpec(memory_space=s...  4.4 us
    ppermute x2, waiting for transfers between devices, to_partner(): return lax.ppermute(send, 'hidden', [(i, i ^ bit) for i in range(peers)])  3.1 us
  transfers between devices with their start and end apart: 3, of which 3 were waited for; matrix products, arithmetic and copies ran while one was open for 0% of the time, Pallas kernels for 0%

profile of v13, /device:TPU:8, one launch (start us, length us, event | category | flops | bytes accessed | tf_op | source)
XLA Modules:
  0.0 79.1 jit_solution(4418293714512702236)
XLA Ops:
  0.6 2.0 %shard_map.59 = (bf16[32,4,1920]{2,1,0:T(4,128)(2,1)}, s32[2,512]{1,0:T(2,128)S(1)}, f32[8,128]{1,0:T(8,128)S(1)}) custom-call(bf16[960,128]{1,0:T(8,128)(2,1)} %table_there.1, s32[4,128]{1,0:T(4,128)} %bitcast.2), custom_call_target="tpu_custom_call" | custom-call | flops 1966080 | bytes 747520 | tf_op jit(solution)/shard_map/pallas_call | solution.py:20
  2.7 0.0 copy-start
  2.7 0.0 copy-start.1
  2.7 10.3 %all-to-all-start = ((bf16[32,4,1920]{2,1,0:T(4,128)(2,1)}), bf16[32,4,1920]{2,1,0:T(4,128)(2,1)S(1)}, u32[]{:S(2)}, u32[]{:S(2)}) async-start(bf16[32,4,1920]{2,1,0:T(4,128)(2,1)} %get-tuple-element.11), calls=%async_computation | async-start | bytes 983040 | tf_op jit(solution)/shard_map/all_to_all | solution.py:34
  13.0 0.0 copy-done
  13.0 0.0 copy-done.1
  13.0 0.2 shard_map.60
  13.3 1.9 %collective-permute-start = (bf16[128,256]{1,0:T(8,128)(2,1)S(1)}, bf16[128,256]{1,0:T(8,128)(2,1)S(1)}, u32[]{:S(2)}, u32[]{:S(2)}) collective-permute-start(bf16[128,256]{1,0:T(8,128)(2,1)S(1)} %get-tuple-element.14), channel_id=1, source_target_pairs={{0,1},{1,0},{2,3},{3,2},{4,5},{5,4},{6,7},{7,6},{8,9},{9,8},{10,11... | collective-permute-start | bytes 196616 | tf_op jit(solution)/shard_map/ppermute | solution.py:257
  15.2 1.2 %collective-permute-done.arrived = bf16[128,256]{1,0:T(8,128)(2,1)S(1)} collective-permute-done((bf16[128,256]{1,0:T(8,128)(2,1)S(1)}, bf16[128,256]{1,0:T(8,128)(2,1)S(1)}, u32[]{:S(2)}, u32[]{:S(2)}) %collective-permute-start) | collective-permute-done | bytes 65568 | tf_op jit(solution)/shard_map/ppermute | solution.py:257
  16.4 4.3 %collective-permute-start.1 = (bf16[128,128]{1,0:T(8,128)(2,1)S(1)}, bf16[128,128]{1,0:T(8,128)(2,1)S(1)}, u32[]{:S(2)}, u32[]{:S(2)}) collective-permute-start(bf16[128,128]{1,0:T(8,128)(2,1)S(1)} %get-tuple-element.16), channel_id=1, source_target_pairs={{0,2},{1,3},{2,0},{3,1},{4,6},{5,7},{6,4},{7,5},{8,10},{9,11},{10,... | collective-permute-start | bytes 98312 | tf_op jit(solution)/shard_map/ppermute | solution.py:257
  20.7 1.9 %collective-permute-done.1.refs_3_ = bf16[128,128]{1,0:T(8,128)(2,1)S(1)} collective-permute-done((bf16[128,128]{1,0:T(8,128)(2,1)S(1)}, bf16[128,128]{1,0:T(8,128)(2,1)S(1)}, u32[]{:S(2)}, u32[]{:S(2)}) %collective-permute-start.1) | collective-permute-done | bytes 32800 | tf_op jit(solution)/shard_map/ppermute | solution.py:257
  22.6 7.4 %all-to-all-done.refs_0_ = bf16[32,4,1920]{2,1,0:T(4,128)(2,1)S(1)} async-done(((bf16[32,4,1920]{2,1,0:T(4,128)(2,1)}), bf16[32,4,1920]{2,1,0:T(4,128)(2,1)S(1)}, u32[]{:S(2)}, u32[]{:S(2)}) %all-to-all-start) | async-done | bytes 491552 | tf_op jit(solution)/shard_map/all_to_all | solution.py:34
  30.0 0.5 shard_map.62
  30.5 19.4 %all_to_all.20.arrived = bf16[16,8,640]{2,1,0:T(8,128)(2,1)S(1)} all-to-all(bf16[16,8,640]{2,1,0:T(8,128)(2,1)S(1)} %shard_map.62), channel_id=1, replica_groups=mesh['vocab'=32,'hidden'=16] {'hidden'}, dimensions={0} | all-to-all | bytes 327680 | tf_op jit(solution)/shard_map/all_to_all | solution.py:34
  49.9 0.2 shard_map.63
  50.1 9.7 %all_to_all.21.refs_0_ = bf16[8,72,128]{2,1,0:T(8,128)(2,1)S(1)} all-to-all(bf16[8,72,128]{2,1,0:T(8,128)(2,1)S(1)} %shard_map.63), channel_id=1, replica_groups={{0,16,128,144,256,272,384,400},{32,48,160,176,288,304,416,432},{64,80,1..., dimensions={0} | all-to-all | bytes 294912 | tf_op jit(solution)/shard_map/all_to_all | solution.py:34
  59.8 0.7 shard_map.64
  60.5 17.9 %all_to_all.22.refs_0_ = bf16[32,40,128]{2,1,0:T(8,128)(2,1)S(1)} all-to-all(bf16[32,40,128]{2,1,0:T(8,128)(2,1)S(1)} %shard_map.64), channel_id=1, replica_groups=mesh['vocab'=32,'hidden'=16] {'vocab'}, dimensions={0} | all-to-all | bytes 655360 | tf_op jit(solution)/shard_map/all_to_all | solution.py:34
  78.4 0.7 shard_map.65
  (1 shorter events, 0.0 us)
Async XLA Ops:
  2.7 10.3 %copy-start = (bf16[512,256]{1,0:T(8,128)(2,1)S(1)}, bf16[512,256]{1,0:T(8,128)(2,1)}, u32[]{:S(2)}) copy-start(bf16[512,256]{1,0:T(8,128)(2,1)} %grad_out.3) | copy-start | bytes 786436
  2.7 10.3 %copy-start.1 = (bf16[128,256]{1,0:T(8,128)(2,1)S(1)}, bf16[128,256]{1,0:T(8,128)(2,1)}, u32[]{:S(2)}) copy-start(bf16[128,256]{1,0:T(8,128)(2,1)} %projection.1) | copy-start | bytes 196612
  2.7 27.3 %all-to-all-start = ((bf16[32,4,1920]{2,1,0:T(4,128)(2,1)}), bf16[32,4,1920]{2,1,0:T(4,128)(2,1)S(1)}, u32[]{:S(2)}, u32[]{:S(2)}) async-start(bf16[32,4,1920]{2,1,0:T(4,128)(2,1)} %get-tuple-element.11), calls=%async_computation | async-start | bytes 983040 | tf_op jit(solution)/shard_map/all_to_all | solution.py:34
  13.3 3.1 %collective-permute-start = (bf16[128,256]{1,0:T(8,128)(2,1)S(1)}, bf16[128,256]{1,0:T(8,128)(2,1)S(1)}, u32[]{:S(2)}, u32[]{:S(2)}) collective-permute-start(bf16[128,256]{1,0:T(8,128)(2,1)S(1)} %get-tuple-element.14), channel_id=1, source_target_pairs={{0,1},{1,0},{2,3},{3,2},{4,5},{5,4},{6,7},{7,6},{8,9},{9,8},{10,11... | collective-permute-start | bytes 196616 | tf_op jit(solution)/shard_map/ppermute | solution.py:257
  16.4 6.2 %collective-permute-start.1 = (bf16[128,128]{1,0:T(8,128)(2,1)S(1)}, bf16[128,128]{1,0:T(8,128)(2,1)S(1)}, u32[]{:S(2)}, u32[]{:S(2)}) collective-permute-start(bf16[128,128]{1,0:T(8,128)(2,1)S(1)} %get-tuple-element.16), channel_id=1, source_target_pairs={{0,2},{1,3},{2,0},{3,1},{4,6},{5,7},{6,4},{7,5},{8,10},{9,11},{10,... | collective-permute-start | bytes 98312 | tf_op jit(solution)/shard_map/ppermute | solution.py:257
